TPU v7x, 256 devices: a whole 4x4x8 slice. The times are simulated.
256 devices in a mesh: scan: 128 (over y_hi, x, z, core), tile: 2 (over y_lo).
Axes of the slice: x: 4, y: 4 (y_hi: 2, y_lo: 2; y = y_hi * 2 + y_lo), z: 8, core: 2. Of those that a mesh axis runs over, the one named last changes fastest.
Arguments:
- probe_modes: float32 [12, 2, 128, 128], replicated, may hold values from -5 to 5
- patterns: float32 [1024, 128, 128], P(('scan', 'tile')), may hold values from 0.005 to 300
- specimen: float32 [2, 16384, 512], P(None, 'scan', 'tile'), may hold values from -17.5 to 17.5
- offsets: int32 [1024, 2], P(('scan', 'tile')), may hold values from -128 to 16384, as said below
Outputs:
- new_probe: float32 [12, 2, 128, 128], replicated
- new_specimen: float32 [2, 16384, 512], P(None, 'scan', 'tile')
Inputs may be any that keep to these rules, and one draw needn't show every extreme that they name: `offsets`: position p lies in aligned block b = p // 4, held by the device of scan index s = b // (the number of tile devices) and tile index t = b % (the number of tile devices); its row offset lies in s * 128 - 128 to s * 128 + 128, its column offset in t * 256 - 128 to t * 256 + 256, both ends included; in every block one position has its row offset at the lower end and its column offset at the upper end, and one has its row offset at the upper end.
All inputs are finite; a program needn't handle non-finite values.
Results may differ from a plain program's by a relative error of at most 0.0001.
Values sent between devices are 32-bit elements; how exact they have to be, the bound alone decides.
A program may use at most 64 MiB of HBM per device.

v0:
```python
import math

import jax
import jax.numpy as jnp
from jax import lax
from jax.sharding import PartitionSpec as P

NS_STEPS = 8


highest = lax.Precision.HIGHEST
light_floor = 0.05
object_reg = 0.5
probe_reg = 1.0
total_eps = 1e-06


def extended_2(array, sides, width):
    for axis, dim in sides:
        size, length = (lax.axis_size(axis), array.shape[dim])
        up = [(i, (i + 1) % size) for i in range(size - 1)]
        down = [(j, i) for i, j in up]
        last = lax.slice_in_dim(array, length - width, length, axis=dim)
        first = lax.slice_in_dim(array, 0, width, axis=dim)
        before = lax.ppermute(last, axis, up)
        after = lax.ppermute(first, axis, down)
        array = jnp.concatenate([before, array, after], axis=dim)
    return array


def dft_tables(detector):
    indices = jnp.arange(detector, dtype=jnp.int32)
    product = indices[:, None] * indices[None, :] % detector
    angles = -2.0 * math.pi / detector * product.astype(jnp.float32)
    norm_factor = 1.0 / math.sqrt(detector)
    return (jnp.cos(angles) * norm_factor, jnp.sin(angles) * norm_factor)


def complex_section(real_part, imag_part, table, direction, on_right):
    stacked = jnp.stack([real_part, imag_part])
    if on_right:
        products = jnp.einsum(
            "cmxy,yw->cmxw", stacked, table, precision=highest, preferred_element_type=jnp.float32
        )
        split_at = real_part.shape[-1]
        plain_re, twist_re = (products[0, :, :, :split_at], products[0, :, :, split_at:])
        plain_im, twist_im = (products[1, :, :, :split_at], products[1, :, :, split_at:])
    else:
        products = jnp.einsum(
            "wx,cmxy->cmwy", table, stacked, precision=highest, preferred_element_type=jnp.float32
        )
        split_at = real_part.shape[-2]
        plain_re, twist_re = (products[0, :, :split_at], products[0, :, split_at:])
        plain_im, twist_im = (products[1, :, :split_at], products[1, :, split_at:])
    return (plain_re - direction * twist_im, direction * twist_re + plain_im)


def newton_steps(gram_re, gram_im):
    mode_count = gram_re.shape[0]
    upper = jnp.concatenate([gram_re, -gram_im], axis=1)
    lower = jnp.concatenate([gram_im, gram_re], axis=1)
    embedded = jnp.concatenate([upper, lower], axis=0)
    frobenius = jnp.sqrt(jnp.sum(embedded * embedded))
    identity = jnp.eye(2 * mode_count, dtype=jnp.float32)
    current = embedded / frobenius
    inverse = identity
    for repeat in range(NS_STEPS):
        factor = 1.5 * identity - 0.5 * jnp.dot(
            inverse, current, precision=highest, preferred_element_type=jnp.float32
        )
        current = jnp.dot(current, factor, precision=highest, preferred_element_type=jnp.float32)
        inverse = jnp.dot(factor, inverse, precision=highest, preferred_element_type=jnp.float32)
    inverse = inverse / jnp.sqrt(frobenius)
    return (inverse[:mode_count, :mode_count], inverse[mode_count:, :mode_count])


def gram_parts(mode_rows):
    real_rows = mode_rows[0::2]
    imag_rows = mode_rows[1::2]
    gram_re = jnp.dot(
        real_rows, real_rows.T, precision=highest, preferred_element_type=jnp.float32
    ) + jnp.dot(imag_rows, imag_rows.T, precision=highest, preferred_element_type=jnp.float32)
    gram_im = jnp.dot(
        real_rows, imag_rows.T, precision=highest, preferred_element_type=jnp.float32
    ) - jnp.dot(imag_rows, real_rows.T, precision=highest, preferred_element_type=jnp.float32)
    return (gram_re, gram_im)


def orthonormal_rows(mode_rows, gram_re, gram_im, power_ratio):
    real_rows = mode_rows[0::2]
    imag_rows = mode_rows[1::2]
    mix_re, mix_im = newton_steps(gram_re, gram_im)
    ortho_re = jnp.dot(
        mix_re.T, real_rows, precision=highest, preferred_element_type=jnp.float32
    ) - jnp.dot(mix_im.T, imag_rows, precision=highest, preferred_element_type=jnp.float32)
    ortho_im = jnp.dot(
        mix_im.T, real_rows, precision=highest, preferred_element_type=jnp.float32
    ) + jnp.dot(mix_re.T, imag_rows, precision=highest, preferred_element_type=jnp.float32)
    weight = jnp.sqrt(power_ratio * jnp.diagonal(gram_re))
    joined = jnp.stack([ortho_re, ortho_im], axis=1) * weight[:, None, None]
    return joined.reshape(mode_rows.shape)


def global_totals(measured, modeled):
    return lax.psum((measured, modeled), ("scan", "tile"))


def fold_interior(frame_sum, folded, detector, block_rows, block_cols):
    rows_end = block_rows + 3 * detector
    cols_end = block_cols + 3 * detector
    centre_rows = slice(2 * detector, 2 * detector + block_rows)
    centre_cols = slice(2 * detector, 2 * detector + block_cols)
    interior = frame_sum[:, detector : detector + block_rows, detector : detector + block_cols]
    interior = interior.at[:, :detector, :].add(folded[:, :detector, centre_cols])
    interior = interior.at[:, block_rows - detector :, :].add(folded[:, rows_end:, centre_cols])
    interior = interior.at[:, :, :detector].add(folded[:, centre_rows, :detector])
    interior = interior.at[:, :, block_cols - detector :].add(folded[:, centre_rows, cols_end:])
    interior = interior.at[:, :detector, :detector].add(folded[:, :detector, :detector])
    interior = interior.at[:, :detector, block_cols - detector :].add(
        folded[:, :detector, cols_end:]
    )
    interior = interior.at[:, block_rows - detector :, :detector].add(
        folded[:, rows_end:, :detector]
    )
    interior = interior.at[:, block_rows - detector :, block_cols - detector :].add(
        folded[:, rows_end:, cols_end:]
    )
    return interior


def body(probe_modes, patterns, specimen, offsets):
    detector = probe_modes.shape[-1]
    mode_count = probe_modes.shape[0]
    block_rows = specimen.shape[1]
    block_cols = specimen.shape[2]
    position_count = patterns.shape[0]
    table_re, table_im = dft_tables(detector)
    right_table = jnp.concatenate([table_re, table_im], axis=1)
    left_table = jnp.concatenate([table_re, table_im], axis=0)
    probe_re = probe_modes[:, 0]
    probe_im = probe_modes[:, 1]
    probe_power = jnp.sum(probe_re * probe_re + probe_im * probe_im, axis=0)
    extended = extended_2(specimen, (("scan", 1), ("tile", 2)), detector)
    row_base = lax.axis_index("scan") * block_rows - detector
    col_base = lax.axis_index("tile") * block_cols - detector
    local_rows = offsets[:, 0] - row_base
    local_cols = offsets[:, 1] - col_base
    zero_index = jnp.zeros((), jnp.int32)
    channels = 3

    def patch_at(position):
        return lax.dynamic_slice(
            extended,
            (zero_index, local_rows[position], local_cols[position]),
            (2, detector, detector),
        )

    def one_position(position, running):
        grad_re, grad_im, light_sum, frame_sum, model_sum = running
        patch_now = patch_at(position)
        patch_re = patch_now[0]
        patch_im = patch_now[1]
        exit_re = probe_re * patch_re[None] - probe_im * patch_im[None]
        exit_im = probe_re * patch_im[None] + probe_im * patch_re[None]
        model_sum = model_sum + jnp.sum(exit_re * exit_re + exit_im * exit_im)
        half_re, half_im = complex_section(exit_re, exit_im, right_table, 1.0, True)
        far_re, far_im = complex_section(half_re, half_im, left_table, 1.0, False)
        model_light = jnp.sum(far_re * far_re + far_im * far_im, axis=0)
        factor = (
            jnp.sqrt(patterns[position]) / jnp.sqrt(jnp.maximum(model_light, light_floor)) - 1.0
        )
        back_re, back_im = complex_section(
            far_re * factor[None], far_im * factor[None], right_table, -1.0, True
        )
        change_re, change_im = complex_section(back_re, back_im, left_table, -1.0, False)
        grad_re = grad_re + patch_re[None] * change_re + patch_im[None] * change_im
        grad_im = grad_im + patch_re[None] * change_im - patch_im[None] * change_re
        light_sum = light_sum + patch_re * patch_re + patch_im * patch_im
        num_re = jnp.sum(probe_re * change_re + probe_im * change_im, axis=0)
        num_im = jnp.sum(probe_re * change_im - probe_im * change_re, axis=0)
        addition = jnp.stack([num_re, num_im, probe_power])
        row_at = local_rows[position]
        col_at = local_cols[position]
        previous = lax.dynamic_slice(
            frame_sum, (zero_index, row_at, col_at), (channels, detector, detector)
        )
        frame_sum = lax.dynamic_update_slice(
            frame_sum, previous + addition, (zero_index, row_at, col_at)
        )
        return (grad_re, grad_im, light_sum, frame_sum, model_sum)

    mode_zeros = jnp.zeros((mode_count, detector, detector), jnp.float32)
    frame_init = jnp.zeros(
        (channels, block_rows + 2 * detector, block_cols + 2 * detector), jnp.float32
    )
    initial = (
        mode_zeros,
        mode_zeros,
        jnp.zeros((detector, detector), jnp.float32),
        frame_init,
        jnp.zeros((), jnp.float32),
    )
    grad_re, grad_im, light_sum, frame_sum, model_sum = lax.fori_loop(
        0, position_count, one_position, initial
    )
    measured_all, model_all = global_totals(jnp.sum(patterns), model_sum)
    power_ratio = measured_all / (model_all + total_eps)
    folded = extended_2(frame_sum, (("scan", 1), ("tile", 2)), detector)
    interior = fold_interior(frame_sum, folded, detector, block_rows, block_cols)
    interior_num = interior[0:2]
    interior_light = interior[2]
    new_specimen = specimen + interior_num / (interior_light + object_reg)[None]
    grad_rows = jnp.stack([grad_re, grad_im], axis=1).reshape(2 * mode_count, -1)
    light_row = light_sum.reshape(1, -1)
    probe_rows = probe_modes.reshape(2 * mode_count, -1)
    grad_total, light_total = lax.psum((grad_rows, light_row), ("scan", "tile"))
    updated = probe_rows + grad_total / (light_total + probe_reg)
    gram_re, gram_im = gram_parts(updated)
    new_probe = orthonormal_rows(updated, gram_re, gram_im, power_ratio).reshape(probe_modes.shape)
    return (new_probe, new_specimen)


def solution(mesh):
    return jax.shard_map(
        body,
        mesh=mesh,
        in_specs=(
            P(),
            P(("scan", "tile"), None, None),
            P(None, "scan", "tile"),
            P(("scan", "tile"), None),
        ),
        out_specs=(P(), P(None, "scan", "tile")),
        check_vma=False,
    )
```

profile of v0, /device:TPU:1, one launch (start us, length us, event | category | flops | bytes accessed | tf_op | source)
XLA Modules:
  0.0 484.5 jit_solution(16248990346696429132)
XLA Ops:
  7.2 5.2 %collective-permute-start.1 = (f32[2,128,256]{2,1,0:T(8,128)}, f32[2,128,256]{2,1,0:T(8,128)S(1)}, u32[]{:S(2)}, u32[]{:S(2)}) collective-permute-start(f32[2,128,256]{2,1,0:T(8,128)} %param.28), channel_id=1, source_target_pairs={{2,0},{4,2},{6,4},{8,6},{10,8},{12,10},{14,12},{16,14},{18,16},{20... | collective-permute-start | bytes 786440 | tf_op jit(solution)/shard_map/ppermute | solution.py:26
  18.2 3.2 collective-permute-start.2
  22.8 9.3 %collective-permute-done.2 = f32[2,384,128]{2,1,0:T(8,128)S(1)} collective-permute-done((f32[2,384,128]{2,1,0:T(8,128)S(1)}, f32[2,384,128]{2,1,0:T(8,128)S(1)}, u32[]{:S(2)}, u32[]{:S(2)}) %collective-permute-start.2) | collective-permute-done | bytes 393248 | tf_op jit(solution)/shard_map/ppermute | solution.py:25
  32.1 4.1 collective-permute-done.3
  39.3 113.3 %while.34 = (s32[]{:T(128)}, f32[12,128,128]{2,1,0:T(8,128)}, f32[12,128,128]{2,1,0:T(8,128)}, f32[128,128]{1,0:T(8,128)}, f32[3,384,512]{2,1,0:T(8,128)}, /*ind...) while((s32[]{:T(128)}, f32[12,128,128]{2,1,0:T(8,128)}, ...), condition=%wide.region_6.7_spmd.clone, body=%wide.region_1.6_spmd.clone.sunk | while | flops 4844257280 | bytes 53870996 | solution.py:203
  49.6 2.8 convolution_bitcast_fusion.4
  52.8 2.8 fusion.164
  55.8 2.7 convolution_bitcast_fusion.5
  63.0 2.8 dynamic_update_slice.12
  76.2 2.8 convolution_bitcast_fusion.4
  79.4 2.8 fusion.164
  82.4 2.7 convolution_bitcast_fusion.5
  87.1 2.8 fusion.166
  91.1 2.8 dynamic_update_slice.12
  101.4 2.7 fusion.162
  104.3 2.8 convolution_bitcast_fusion.4
  107.5 2.8 fusion.164
  110.5 2.7 convolution_bitcast_fusion.5
  115.2 2.8 fusion.166
  119.2 4.0 dynamic_update_slice.12
  133.6 2.8 convolution_bitcast_fusion.4
  136.8 2.8 fusion.164
  139.8 2.7 convolution_bitcast_fusion.5
  144.5 2.8 fusion.166
  148.5 4.1 dynamic_update_slice.12
  152.6 2.8 fusion.66
  163.8 89.6 %all-reduce = (f32[]{:T(128)}, f32[]{:T(128)}) all-reduce(f32[]{:T(128)} %reduce_sum.93, f32[]{:T(128)} %get-tuple-element.473), channel_id=1, replica_groups=mesh['scan'=128,'tile'=2] {'scan','tile'}, use_global_device_ids=true, to_apply=%region_11.12 | all-reduce | flops 2 | bytes 16 | tf_op jit(solution)/shard_map/psum | solution.py:105
  260.8 5.9 %collective-permute-start.6 = (f32[3,640,128]{2,1,0:T(8,128)}, f32[3,640,128]{2,1,0:T(8,128)}, u32[]{:S(2)}, u32[]{:S(2)}) collective-permute-start(f32[3,640,128]{2,1,0:T(8,128)} %get-tuple-element.606), channel_id=1, source_target_pairs={{0,1},{2,3},{4,5},{6,7},{8,9},{10,11},{12,13},{14,15},{16,17},{18,... | collective-permute-start | bytes 2949128 | tf_op jit(solution)/shard_map/ppermute | solution.py:25
  267.8 166.1 %all-reduce.4.cloned.1.call-done = (f32[24,16384]{1,0:T(8,128)}, f32[1,16384]{1,0:T(1,128)}) async-done(((f32[24,16384]{1,0:T(8,128)}, f32[1,16384]{1,0:T(1,128)}), (f32[24,16384]{1,0:T(8,128)}, f32[1,16384]{1,0:T(1,128)})) %all-reduce.4.cloned.1.call-update) | async-done | bytes 1638416 | tf_op jit(solution)/shard_map/psum | solution.py:216
  434.8 3.5 bitcast_add_fusion
  438.3 5.7 %slice.446 = f32[12,16384]{1,0:T(8,128)S(1)} slice(f32[24,16384]{1,0:T(8,128)} %bitcast_add_fusion), slice={[1:24:2], [0:16384:1]} | slice | bytes 1572864 | tf_op jit(solution)/shard_map/slice | solution.py:79
  444.0 5.7 %slice.445 = f32[12,16384]{1,0:T(8,128)S(1)} slice(f32[24,16384]{1,0:T(8,128)} %bitcast_add_fusion), slice={[0:24:2], [0:16384:1]} | slice | bytes 1572864 | tf_op jit(solution)/shard_map/slice | solution.py:78
  (178 shorter events, 92.4 us)
Async XLA Ops:
  7.2 10.9 %copy-start.10 = (f32[2,128,256]{2,1,0:T(8,128)S(1)}, f32[2,128,256]{2,1,0:T(8,128)}, u32[]{:S(2)}) copy-start(f32[2,128,256]{2,1,0:T(8,128)} %param.28) | copy-start | bytes 786436
  7.2 426.7 %all-reduce.4.cloned.1.call-start = ((), (), s32[]{:S(2)}) async-start(), calls=%async_computation | async-start | bytes 3276800 | tf_op jit(solution)/shard_map/psum | solution.py:216
  7.2 10.9 %collective-permute-start.1 = (f32[2,128,256]{2,1,0:T(8,128)}, f32[2,128,256]{2,1,0:T(8,128)S(1)}, u32[]{:S(2)}, u32[]{:S(2)}) collective-permute-start(f32[2,128,256]{2,1,0:T(8,128)} %param.28), channel_id=1, source_target_pairs={{2,0},{4,2},{6,4},{8,6},{10,8},{12,10},{14,12},{16,14},{18,16},{20... | collective-permute-start | bytes 786440 | tf_op jit(solution)/shard_map/ppermute | solution.py:26
  12.5 5.5 %collective-permute-start = (f32[2,128,256]{2,1,0:T(8,128)}, f32[2,128,256]{2,1,0:T(8,128)S(1)}, u32[]{:S(2)}, u32[]{:S(2)}) collective-permute-start(f32[2,128,256]{2,1,0:T(8,128)} %param.28), channel_id=1, source_target_pairs={{0,2},{2,4},{4,6},{6,8},{8,10},{10,12},{12,14},{14,16},{16,18},{18... | collective-permute-start | bytes 786440 | tf_op jit(solution)/shard_map/ppermute | solution.py:25
  18.0 4.6 copy-start.2
  18.2 14.0 %collective-permute-start.2 = (f32[2,384,128]{2,1,0:T(8,128)S(1)}, f32[2,384,128]{2,1,0:T(8,128)S(1)}, u32[]{:S(2)}, u32[]{:S(2)}) collective-permute-start(f32[2,384,128]{2,1,0:T(8,128)S(1)} %get-tuple-element.611), channel_id=1, source_target_pairs={{0,1},{2,3},{4,5},{6,7},{8,9},{10,11},{12,13},{14,15},{16,17},{18,... | collective-permute-start | bytes 1179656 | tf_op jit(solution)/shard_map/ppermute | solution.py:25
  21.4 14.9 %collective-permute-start.3 = (f32[2,384,128]{2,1,0:T(8,128)S(1)}, f32[2,384,128]{2,1,0:T(8,128)S(1)}, u32[]{:S(2)}, u32[]{:S(2)}) collective-permute-start(f32[2,384,128]{2,1,0:T(8,128)S(1)} %get-tuple-element.612), channel_id=1, source_target_pairs={{1,0},{3,2},{5,4},{7,6},{9,8},{11,10},{13,12},{15,14},{17,16},{19,... | collective-permute-start | bytes 1179656 | tf_op jit(solution)/shard_map/ppermute | solution.py:26
  60.5 1.4 copy-start.4
  60.5 1.4 copy-start.5
  87.1 2.8 copy-start.4
  87.1 2.8 copy-start.5
  115.2 2.8 copy-start.4
  115.2 2.8 copy-start.5
  144.5 2.8 copy-start.4
  144.5 2.8 copy-start.5
  152.6 8.9 %copy-start = (f32[12,128,128]{2,1,0:T(8,128)S(1)}, f32[12,128,128]{2,1,0:T(8,128)}, u32[]{:S(2)}) copy-start(f32[12,128,128]{2,1,0:T(8,128)} %get-tuple-element.471) | copy-start | bytes 2359300
  152.6 8.9 %copy-start.1 = (f32[12,128,128]{2,1,0:T(8,128)S(1)}, f32[12,128,128]{2,1,0:T(8,128)}, u32[]{:S(2)}) copy-start(f32[12,128,128]{2,1,0:T(8,128)} %get-tuple-element.470) | copy-start | bytes 2359300
  155.4 99.3 %collective-permute-start.4 = (f32[3,128,512]{2,1,0:T(8,128)}, f32[3,128,512]{2,1,0:T(8,128)S(1)}, u32[]{:S(2)}, u32[]{:S(2)}) collective-permute-start(f32[3,128,512]{2,1,0:T(8,128)} %get-tuple-element.607), channel_id=1, source_target_pairs={{0,2},{2,4},{4,6},{6,8},{8,10},{10,12},{12,14},{14,16},{16,18},{18... | collective-permute-start | bytes 2359304 | tf_op jit(solution)/shard_map/ppermute | solution.py:25
  157.3 99.6 %collective-permute-start.5 = (f32[3,128,512]{2,1,0:T(8,128)}, f32[3,128,512]{2,1,0:T(8,128)S(1)}, u32[]{:S(2)}, u32[]{:S(2)}) collective-permute-start(f32[3,128,512]{2,1,0:T(8,128)} %get-tuple-element.608), channel_id=1, source_target_pairs={{2,0},{4,2},{6,4},{8,6},{10,8},{12,10},{14,12},{16,14},{18,16},{20... | collective-permute-start | bytes 2359304 | tf_op jit(solution)/shard_map/ppermute | solution.py:26
  254.7 2.2 copy-start.7
  256.9 1.0 copy-start.9
  257.9 8.8 %copy-start.8 = (f32[3,128,512]{2,1,0:T(8,128)S(1)}, f32[3,128,512]{2,1,0:T(8,128)}, u32[]{:S(2)}) copy-start(f32[3,128,512]{2,1,0:T(8,128)} %copy-done.7) | copy-start | bytes 2359300
  259.3 175.4 %copy-start.3 = (f32[12,2,128,128]{3,2,1,0:T(8,128)S(1)}, f32[12,2,128,128]{3,2,1,0:T(8,128)}, u32[]{:S(2)}) copy-start(f32[12,2,128,128]{3,2,1,0:T(8,128)} %param.26) | copy-start | bytes 4718596
  259.3 212.6 %collective-permute-start.7 = (f32[3,640,128]{2,1,0:T(8,128)}, f32[3,640,128]{2,1,0:T(8,128)}, u32[]{:S(2)}, u32[]{:S(2)}) collective-permute-start(f32[3,640,128]{2,1,0:T(8,128)} %get-tuple-element.605), channel_id=1, source_target_pairs={{1,0},{3,2},{5,4},{7,6},{9,8},{11,10},{13,12},{15,14},{17,16},{19,... | collective-permute-start | bytes 2949128 | tf_op jit(solution)/shard_map/ppermute | solution.py:26
  260.8 210.2 %collective-permute-start.6 = (f32[3,640,128]{2,1,0:T(8,128)}, f32[3,640,128]{2,1,0:T(8,128)}, u32[]{:S(2)}, u32[]{:S(2)}) collective-permute-start(f32[3,640,128]{2,1,0:T(8,128)} %get-tuple-element.606), channel_id=1, source_target_pairs={{0,1},{2,3},{4,5},{6,7},{8,9},{10,11},{12,13},{14,15},{16,17},{18,... | collective-permute-start | bytes 2949128 | tf_op jit(solution)/shard_map/ppermute | solution.py:25
  465.6 2.4 copy-start.6
  471.9 5.0 %copy-start.11 = (f32[2,128,256]{2,1,0:T(8,128)S(1)}, f32[2,128,256]{2,1,0:T(8,128)}, u32[]{:S(2)}) copy-start(f32[2,128,256]{2,1,0:T(8,128)} %param.28) | copy-start | bytes 786436
Sparse Core Ops, SparseCore 0:
  163.9 269.8 all-reduce.3
where the time goes:
time: 488 us; the launch traced here: 485 us
  waiting for transfers between devices  180 us (37%)
  blocking collectives  89.6 us (18%)
  matrix products  60.8 us (12%)
  other arithmetic  51.5 us (11%)
  local copies, waits for them, and re-layouts  46.4 us (10%)
  starting transfers between devices  23.3 us (5%)
  between operations  16.5 us (3%)
  loops' own time  16.4 us (3%)
    psum x1, waiting for transfers between devices, body(): grad_total, light_total = lax.psum((grad_rows, light_row), ('scan', 'tile'))  166 us
    psum x1, blocking collectives, global_totals(): return lax.psum((measured, modeled), ('scan', 'tile'))  89.6 us
    dot_general x8, matrix products, complex_section(): jnp.einsum('wx,cmxy->cmwy', table, stacked, precision=highest, preferred_...  22 us
    dot_general x8, matrix products, complex_section(): jnp.einsum('cmxy,yw->cmxw', stacked, table, precision=highest, preferred_...  21.8 us
    another operation x1, loops' own time, body(): lax.fori_loop(0, position_count, one_position, initial)  16.4 us
    dynamic_update_slice x4, local copies, waits for them, and re-layouts, one_position(): lax.dynamic_update_slice(frame_sum, previous + addition, (zero_index, row...  13.8 us
    ppermute x4, starting transfers between devices, extended_2(): before = lax.ppermute(last, axis, up)  12.9 us
    ppermute x4, starting transfers between devices, extended_2(): after = lax.ppermute(first, axis, down)  10.4 us
  transfers between devices with their start and end apart: 9, of which 4 were waited for; matrix products, arithmetic and copies ran while one was open for 10% of the time, Pallas kernels for 0%

commit v1 on v0

v1 whole, which is shorter than its diff:
```python
import math

import jax
import jax.numpy as jnp
import ml_dtypes
import numpy as np
from jax import lax
from jax.experimental import pallas as pl
from jax.experimental.pallas import tpu as pltpu
from jax.sharding import PartitionSpec as P

NS_STEPS = 8
DET = 128
TALL = 136
LIGHT_FLOOR = 0.05
OBJECT_REG = 0.5
PROBE_REG = 1.0
TOTAL_EPS = 1e-06
VMEM = pl.BlockSpec(memory_space=pltpu.VMEM)
SMEM = pl.BlockSpec(memory_space=pltpu.SMEM)
highest = lax.Precision.HIGHEST


def split_tables():
    index = np.arange(DET)
    angles = -2.0 * math.pi / DET * (index[:, None] * index[None, :] % DET)
    cos, sin = np.cos(angles) / math.sqrt(DET), np.sin(angles) / math.sqrt(DET)
    right = np.block([[cos, sin], [-sin, cos]])
    tables = []
    for matrix in (right, right.T):
        high = matrix.astype(ml_dtypes.bfloat16)
        low = (matrix - high.astype(np.float64)).astype(ml_dtypes.bfloat16)
        tables += [high, low]
    return [jnp.asarray(table) for table in tables]


def split(value):
    high = value.astype(jnp.bfloat16)
    return high, (value - high.astype(jnp.float32)).astype(jnp.bfloat16)


def mm(a, b):
    return jnp.dot(a, b, preferred_element_type=jnp.float32)


def window_of(local_ref, position):
    row = local_ref[position, 0]
    col = local_ref[position, 1]
    tile = jnp.minimum(col // DET, 2)
    slab = jnp.minimum(row // 8, 31)
    return pl.multiple_of(slab * 8, 8), row - slab * 8, pl.multiple_of(tile * DET, DET), col - tile * DET


def positions_kernel(
    local_ref,
    probe_ref,
    patterns_ref,
    ext_ref,
    rh_ref,
    rl_ref,
    lh_ref,
    ll_ref,
    sums_ref,
    frame_ref,
    patch_ref,
    far_ref,
    num_ref,
):
    modes = probe_ref.shape[0]
    pairs = modes // 2
    power = jnp.zeros((DET, DET), jnp.float32)
    for k in range(modes):
        power = power + probe_ref[k, 0] * probe_ref[k, 0] + probe_ref[k, 1] * probe_ref[k, 1]
    sums_ref[...] = jnp.zeros_like(sums_ref)
    frame_ref[...] = jnp.zeros_like(frame_ref)

    def one_position(position, _):
        slab, drop, tile, shift = window_of(local_ref, position)
        for c in range(2):
            window = ext_ref[c, pl.ds(slab, TALL), pl.ds(tile, 2 * DET)]
            window = pltpu.roll(window, lax.rem(2 * DET - shift, 2 * DET), 1)[:, :DET]
            patch_ref[c] = pltpu.roll(window, lax.rem(TALL - drop, TALL), 0)[:DET]
        model = jnp.zeros((DET, DET), jnp.float32)
        for j in range(pairs):
            lefts = []
            for k in (2 * j, 2 * j + 1):
                pr, pi = probe_ref[k, 0], probe_ref[k, 1]
                ar, ai = patch_ref[0], patch_ref[1]
                lefts.append(jnp.concatenate([pr * ar - pi * ai, pr * ai + pi * ar], axis=1))
            xh, xl = split(jnp.concatenate(lefts, axis=0))
            half = mm(xh, rh_ref[...]) + mm(xl, rh_ref[...]) + mm(xh, rl_ref[...])
            half = jnp.concatenate(
                [
                    jnp.concatenate([half[:DET, :DET], half[DET:, :DET]], axis=1),
                    jnp.concatenate([half[:DET, DET:], half[DET:, DET:]], axis=1),
                ],
                axis=0,
            )
            yh, yl = split(half)
            far = mm(lh_ref[...], yh) + mm(lh_ref[...], yl) + mm(ll_ref[...], yh)
            far_ref[j] = far
            squares = far * far
            squares = squares[:DET] + squares[DET:]
            model = model + squares[:, :DET] + squares[:, DET:]
        factor = jnp.sqrt(patterns_ref[position]) / jnp.sqrt(jnp.maximum(model, LIGHT_FLOOR)) - 1.0
        wide = jnp.concatenate([factor, factor], axis=1)
        wide = jnp.concatenate([wide, wide], axis=0)
        num_ref[...] = jnp.zeros_like(num_ref)
        for j in range(pairs):
            bh, bl = split(far_ref[j] * wide)
            back = mm(rh_ref[...], bh) + mm(rh_ref[...], bl) + mm(rl_ref[...], bh)
            back = jnp.concatenate(
                [
                    jnp.concatenate([back[:DET, :DET], back[DET:, :DET]], axis=1),
                    jnp.concatenate([back[:DET, DET:], back[DET:, DET:]], axis=1),
                ],
                axis=0,
            )
            zh, zl = split(back)
            change = mm(zh, lh_ref[...]) + mm(zl, lh_ref[...]) + mm(zh, ll_ref[...])
            for i in range(2):
                k = 2 * j + i
                cr, ci = change[i * DET : i * DET + DET, :DET], change[i * DET : i * DET + DET, DET:]
                pr, pi = probe_ref[k, 0], probe_ref[k, 1]
                ar, ai = patch_ref[0], patch_ref[1]
                sums_ref[2 * k] += ar * cr + ai * ci
                sums_ref[2 * k + 1] += ar * ci - ai * cr
                num_ref[0] += pr * cr + pi * ci
                num_ref[1] += pr * ci - pi * cr
        ar, ai = patch_ref[0], patch_ref[1]
        sums_ref[2 * modes] += ar * ar + ai * ai
        sums_ref[2 * modes + 1] += patterns_ref[position]
        for c in range(3):
            value = num_ref[c] if c < 2 else power
            value = jnp.concatenate([value, jnp.zeros((8, DET), jnp.float32)], axis=0)
            value = pltpu.roll(value, drop, 0)
            value = jnp.concatenate([value, jnp.zeros_like(value)], axis=1)
            frame_ref[c, pl.ds(slab, TALL), pl.ds(tile, 2 * DET)] += pltpu.roll(value, shift, 1)
        return 0

    lax.fori_loop(0, patterns_ref.shape[0], one_position, 0)


def positions(local, probe, patterns, extended):
    modes = probe.shape[0]
    return pl.pallas_call(
        positions_kernel,
        out_shape=(
            jax.ShapeDtypeStruct((2 * modes + 2, DET, DET), jnp.float32),
            jax.ShapeDtypeStruct((3,) + extended.shape[1:], jnp.float32),
        ),
        in_specs=[SMEM] + [VMEM] * 7,
        out_specs=(VMEM, VMEM),
        scratch_shapes=[
            pltpu.VMEM((2, DET, DET), jnp.float32),
            pltpu.VMEM((modes // 2, 2 * DET, 2 * DET), jnp.float32),
            pltpu.VMEM((2, DET, DET), jnp.float32),
        ],
        name="positions",
    )(local, probe, patterns, extended, *split_tables())


def extended_2(array, sides, width):
    for axis, dim in sides:
        size, length = (lax.axis_size(axis), array.shape[dim])
        up = [(i, (i + 1) % size) for i in range(size - 1)]
        down = [(j, i) for i, j in up]
        last = lax.slice_in_dim(array, length - width, length, axis=dim)
        first = lax.slice_in_dim(array, 0, width, axis=dim)
        before = lax.ppermute(last, axis, up)
        after = lax.ppermute(first, axis, down)
        array = jnp.concatenate([before, array, after], axis=dim)
    return array


def newton_steps(gram_re, gram_im):
    mode_count = gram_re.shape[0]
    upper = jnp.concatenate([gram_re, -gram_im], axis=1)
    lower = jnp.concatenate([gram_im, gram_re], axis=1)
    embedded = jnp.concatenate([upper, lower], axis=0)
    frobenius = jnp.sqrt(jnp.sum(embedded * embedded))
    identity = jnp.eye(2 * mode_count, dtype=jnp.float32)
    current = embedded / frobenius
    inverse = identity
    for repeat in range(NS_STEPS):
        factor = 1.5 * identity - 0.5 * jnp.dot(
            inverse, current, precision=highest, preferred_element_type=jnp.float32
        )
        current = jnp.dot(current, factor, precision=highest, preferred_element_type=jnp.float32)
        inverse = jnp.dot(factor, inverse, precision=highest, preferred_element_type=jnp.float32)
    inverse = inverse / jnp.sqrt(frobenius)
    return (inverse[:mode_count, :mode_count], inverse[mode_count:, :mode_count])


def gram_parts(mode_rows):
    real_rows = mode_rows[0::2]
    imag_rows = mode_rows[1::2]
    gram_re = jnp.dot(
        real_rows, real_rows.T, precision=highest, preferred_element_type=jnp.float32
    ) + jnp.dot(imag_rows, imag_rows.T, precision=highest, preferred_element_type=jnp.float32)
    gram_im = jnp.dot(
        real_rows, imag_rows.T, precision=highest, preferred_element_type=jnp.float32
    ) - jnp.dot(imag_rows, real_rows.T, precision=highest, preferred_element_type=jnp.float32)
    return (gram_re, gram_im)


def orthonormal_rows(mode_rows, gram_re, gram_im, power_ratio):
    real_rows = mode_rows[0::2]
    imag_rows = mode_rows[1::2]
    mix_re, mix_im = newton_steps(gram_re, gram_im)
    ortho_re = jnp.dot(
        mix_re.T, real_rows, precision=highest, preferred_element_type=jnp.float32
    ) - jnp.dot(mix_im.T, imag_rows, precision=highest, preferred_element_type=jnp.float32)
    ortho_im = jnp.dot(
        mix_im.T, real_rows, precision=highest, preferred_element_type=jnp.float32
    ) + jnp.dot(mix_re.T, imag_rows, precision=highest, preferred_element_type=jnp.float32)
    weight = jnp.sqrt(power_ratio * jnp.diagonal(gram_re))
    joined = jnp.stack([ortho_re, ortho_im], axis=1) * weight[:, None, None]
    return joined.reshape(mode_rows.shape)


def fold_interior(frame_sum, folded, detector, block_rows, block_cols):
    rows_end = block_rows + 3 * detector
    cols_end = block_cols + 3 * detector
    centre_rows = slice(2 * detector, 2 * detector + block_rows)
    centre_cols = slice(2 * detector, 2 * detector + block_cols)
    interior = frame_sum[:, detector : detector + block_rows, detector : detector + block_cols]
    interior = interior.at[:, :detector, :].add(folded[:, :detector, centre_cols])
    interior = interior.at[:, block_rows - detector :, :].add(folded[:, rows_end:, centre_cols])
    interior = interior.at[:, :, :detector].add(folded[:, centre_rows, :detector])
    interior = interior.at[:, :, block_cols - detector :].add(folded[:, centre_rows, cols_end:])
    interior = interior.at[:, :detector, :detector].add(folded[:, :detector, :detector])
    interior = interior.at[:, :detector, block_cols - detector :].add(
        folded[:, :detector, cols_end:]
    )
    interior = interior.at[:, block_rows - detector :, :detector].add(
        folded[:, rows_end:, :detector]
    )
    interior = interior.at[:, block_rows - detector :, block_cols - detector :].add(
        folded[:, rows_end:, cols_end:]
    )
    return interior


def body(probe_modes, patterns, specimen, offsets):
    mode_count = probe_modes.shape[0]
    block_rows, block_cols = specimen.shape[1:]
    sides = (("scan", 1), ("tile", 2))
    extended = extended_2(specimen, sides, DET)
    base = jnp.stack(
        [
            lax.axis_index("scan") * block_rows - DET,
            lax.axis_index("tile") * block_cols - DET,
        ]
    )
    sums, frame_sum = positions(offsets - base, probe_modes, patterns, extended)
    folded = extended_2(frame_sum, sides, DET)
    interior = fold_interior(frame_sum, folded, DET, block_rows, block_cols)
    new_specimen = specimen + interior[0:2] / (interior[2] + OBJECT_REG)[None]
    totals = lax.psum(sums.reshape(2 * mode_count + 2, -1), ("scan", "tile"))
    probe_rows = probe_modes.reshape(2 * mode_count, -1)
    light = totals[2 * mode_count : 2 * mode_count + 1]
    updated = probe_rows + totals[: 2 * mode_count] / (light + PROBE_REG)
    power = jnp.sum(probe_rows * probe_rows, axis=0)
    power_ratio = jnp.sum(totals[2 * mode_count + 1]) / (jnp.sum(power * light[0]) + TOTAL_EPS)
    gram_re, gram_im = gram_parts(updated)
    new_probe = orthonormal_rows(updated, gram_re, gram_im, power_ratio).reshape(probe_modes.shape)
    return (new_probe, new_specimen)


def solution(mesh):
    return jax.shard_map(
        body,
        mesh=mesh,
        in_specs=(
            P(),
            P(("scan", "tile"), None, None),
            P(None, "scan", "tile"),
            P(("scan", "tile"), None),
        ),
        out_specs=(P(), P(None, "scan", "tile")),
        check_vma=False,
    )
```

time: 488 us -> 388 us (0.80)
  blocking collectives: 89.6 us -> 0 us
  waiting for transfers between devices: 180 us -> 267 us
  matrix products: 60.8 us -> 15.9 us
  other arithmetic: 51.5 us -> 16.9 us
  local copies, waits for them, and re-layouts: 46.4 us -> 24 us
  Pallas kernels: 0 us -> 19.5 us
  loops' own time: 16.4 us -> 0 us
    psum x1 -> x0, blocking collectives: 89.6 us -> none  [global_totals(): return lax.psum((measured, modeled), ('scan', 'tile'))]
    psum x1, waiting for transfers between devices: 166 us -> 248 us  [body(): totals = lax.psum(sums.reshape(2 * mode_count + 2, -1), ('scan', 'tile'))]
    dot_general x16 -> x0, matrix products: 43.8 us -> none  [the longest x8 22 us: complex_section(): jnp.einsum('wx,cmxy->cmwy', table, stacked, precision=highest, preferred_...]
    pallas_call x0 -> x1, Pallas kernels: none -> 19.5 us  [positions(): pl.pallas_call(positions_kernel, out_shape=(jax.ShapeDtypeStruct((2 * mod...]
    another operation x1 -> x0, loops' own time: 16.4 us -> none  [body(): lax.fori_loop(0, position_count, one_position, initial)]
    dynamic_update_slice x4 -> x0, local copies, waits for them, and re-layouts: 13.8 us -> none  [one_position(): lax.dynamic_update_slice(frame_sum, previous + addition, (zero_index, row...]
    add x11 -> x2, other arithmetic: 16.7 us -> 3.12 us  [the longest x1 2.37 us: body(): updated = probe_rows + totals[:2 * mode_count] / (light + PROBE_REG)]
    sub x17 -> x1, other arithmetic: 13 us -> 0.58 us  [body(): sums, frame_sum = positions(offsets - base, probe_modes, patterns, extended)]
  transfers between devices with their start and end apart: 9 -> 9, of which waited for: 4 -> 7; matrix products, arithmetic and copies ran while one was open for 10% -> 12% of each run, Pallas kernels for 0% -> 0%
where the time goes in v1:
time: 388 us; the launch traced here: 386 us
  waiting for transfers between devices  267 us (69%)
  starting transfers between devices  26.4 us (7%)
  local copies, waits for them, and re-layouts  24 us (6%)
  Pallas kernels  19.5 us (5%)
  other arithmetic  16.9 us (4%)
  between operations  16.5 us (4%)
  matrix products  15.9 us (4%)
    psum x1, waiting for transfers between devices, body(): totals = lax.psum(sums.reshape(2 * mode_count + 2, -1), ('scan', 'tile'))  248 us
    ppermute x4, starting transfers between devices, extended_2(): before = lax.ppermute(last, axis, up)  20 us
    pallas_call x1, Pallas kernels, positions(): pl.pallas_call(positions_kernel, out_shape=(jax.ShapeDtypeStruct((2 * mod...  19.5 us
    ppermute x4, waiting for transfers between devices, extended_2(): before = lax.ppermute(last, axis, up)  9.53 us
    ppermute x4, waiting for transfers between devices, extended_2(): after = lax.ppermute(first, axis, down)  9.08 us
    unnamed x25, local copies, waits for them, and re-layouts  8.34 us
  transfers between devices with their start and end apart: 9, of which 7 were waited for; matrix products, arithmetic and copies ran while one was open for 12% of the time, Pallas kernels for 0%

profile of v1, /device:TPU:1, one launch (start us, length us, event | category | flops | bytes accessed | tf_op | source)
XLA Modules:
  0.0 386.2 jit_solution(10221899367179138268)
XLA Ops:
  7.2 4.9 %collective-permute-start = (f32[2,128,256]{2,1,0:T(8,128)}, f32[2,128,256]{2,1,0:T(8,128)S(1)}, u32[]{:S(2)}, u32[]{:S(2)}) collective-permute-start(f32[2,128,256]{2,1,0:T(8,128)} %param.30), channel_id=1, source_target_pairs={{0,2},{2,4},{4,6},{6,8},{8,10},{10,12},{12,14},{14,16},{16,18},{18... | collective-permute-start | bytes 786440 | tf_op jit(solution)/shard_map/ppermute | solution.py:170
  12.2 1.9 collective-permute-start.1
  14.1 1.7 collective-permute-done
  16.8 3.3 collective-permute-done.1
  20.1 3.2 collective-permute-start.2
  23.4 1.3 collective-permute-start.3
  25.4 4.1 %collective-permute-done.2 = f32[2,384,128]{2,1,0:T(8,128)S(1)} collective-permute-done((f32[2,384,128]{2,1,0:T(8,128)S(1)}, f32[2,384,128]{2,1,0:T(8,128)S(1)}, u32[]{:S(2)}, u32[]{:S(2)}) %collective-permute-start.2) | collective-permute-done | bytes 393248 | tf_op jit(solution)/shard_map/ppermute | solution.py:170
  29.6 3.0 collective-permute-done.3
  32.6 1.3 pad_maximum_fusion.ext_ref
  33.9 19.5 %positions.1 = (f32[26,128,128]{2,1,0:T(8,128)}, f32[3,384,512]{2,1,0:T(8,128)}) custom-call(s32[4,2]{1,0:T(4,128)} %broadcast_subtract_fusion.local_ref, f32[12,2,128,128]{3,2,1,0:T(8,128)} %probe_ref.1, f32[4,128,128]{2,1,0:T(8,128)} %patterns_ref.1, f32[2,384,512]{2,1,0:T(8,128)} %pad_maximum_fusion.ext_ref, bf16[256,256]{1,0:T(8,128)(2,1)} %constant.240.clone.rh_ref, ...), custom_call_target="tpu_custom_call" | custom-call | tf_op jit(solution)/shard_map/positions/pallas_call | solution.py:146
  53.4 2.9 fusion.25
  56.2 5.9 %collective-permute-start.4 = (f32[3,128,512]{2,1,0:T(8,128)}, f32[3,128,512]{2,1,0:T(8,128)S(1)}, u32[]{:S(2)}, u32[]{:S(2)}) collective-permute-start(f32[3,128,512]{2,1,0:T(8,128)} %get-tuple-element.122), channel_id=1, source_target_pairs={{0,2},{2,4},{4,6},{6,8},{8,10},{10,12},{12,14},{14,16},{16,18},{18... | collective-permute-start | bytes 2359304 | tf_op jit(solution)/shard_map/ppermute | solution.py:170
  62.2 1.9 collective-permute-start.5
  65.1 2.6 copy.17
  67.7 3.7 collective-permute-done.4
  71.5 1.9 constant_dynamic-update-slice_fusion.4
  73.3 2.8 collective-permute-done.5
  76.2 1.5 fusion.24
  77.6 1.3 collective-permute-start.7
  78.9 5.9 %collective-permute-start.6 = (f32[3,640,128]{2,1,0:T(8,128)}, f32[3,640,128]{2,1,0:T(8,128)}, u32[]{:S(2)}, u32[]{:S(2)}) collective-permute-start(f32[3,640,128]{2,1,0:T(8,128)} %get-tuple-element.121), channel_id=1, source_target_pairs={{0,1},{2,3},{4,5},{6,7},{8,9},{10,11},{12,13},{14,15},{16,17},{18,... | collective-permute-start | bytes 2949128 | tf_op jit(solution)/shard_map/ppermute | solution.py:170
  85.9 248.3 %all-reduce.2.cloned.1.call-done = f32[26,16384]{1,0:T(8,128)} async-done(((f32[26,16384]{1,0:T(8,128)}), f32[26,16384]{1,0:T(8,128)}) %all-reduce.2.cloned.1.call-update) | async-done | bytes 1703952 | tf_op jit(solution)/shard_map/psum | solution.py:260
  334.2 2.0 multiply_reduce_fusion.1
  336.3 2.4 bitcast_add_fusion
  339.8 4.6 %slice.261 = f32[12,16384]{1,0:T(8,128)S(1)} slice(f32[24,16384]{1,0:T(8,128)S(1)} %bitcast_add_fusion), slice={[1:24:2], [0:16384:1]} | slice | bytes 1572864 | tf_op jit(solution)/shard_map/slice | solution.py:197
  344.4 5.7 %slice.260 = f32[12,16384]{1,0:T(8,128)S(1)} slice(f32[24,16384]{1,0:T(8,128)} %copy-done.1), slice={[0:24:2], [0:16384:1]} | slice | bytes 1572864 | tf_op jit(solution)/shard_map/slice | solution.py:196
  350.1 1.5 fusion.28
  351.6 1.4 fusion.29
  353.0 1.6 convolution_add_fusion.1
  354.7 1.4 fusion.27
  361.2 2.0 fusion.17
  365.0 2.3 convolution_add_fusion
  371.3 1.4 maximum_multiply_fusion
  (72 shorter events, 20.5 us)
Async XLA Ops:
  7.2 17.5 %copy-start.7 = (s32[4,2]{0,1:T(2,128)S(1)}, s32[4,2]{0,1:T(2,128)}, u32[]{:S(2)}) copy-start(s32[4,2]{0,1:T(2,128)} %param.31) | copy-start | bytes 100
  7.2 327.1 %all-reduce.2.cloned.1.call-start = ((), (), s32[]{:S(2)}) async-start(), calls=%async_computation | async-start | bytes 4194304 | tf_op jit(solution)/shard_map/psum | solution.py:260
  7.2 8.5 %collective-permute-start = (f32[2,128,256]{2,1,0:T(8,128)}, f32[2,128,256]{2,1,0:T(8,128)S(1)}, u32[]{:S(2)}, u32[]{:S(2)}) collective-permute-start(f32[2,128,256]{2,1,0:T(8,128)} %param.30), channel_id=1, source_target_pairs={{0,2},{2,4},{4,6},{6,8},{8,10},{10,12},{12,14},{14,16},{16,18},{18... | collective-permute-start | bytes 786440 | tf_op jit(solution)/shard_map/ppermute | solution.py:170
  12.2 7.9 %collective-permute-start.1 = (f32[2,128,256]{2,1,0:T(8,128)}, f32[2,128,256]{2,1,0:T(8,128)S(1)}, u32[]{:S(2)}, u32[]{:S(2)}) collective-permute-start(f32[2,128,256]{2,1,0:T(8,128)} %param.30), channel_id=1, source_target_pairs={{2,0},{4,2},{6,4},{8,6},{10,8},{12,10},{14,12},{16,14},{18,16},{20... | collective-permute-start | bytes 786440 | tf_op jit(solution)/shard_map/ppermute | solution.py:171
  20.1 9.4 %collective-permute-start.2 = (f32[2,384,128]{2,1,0:T(8,128)S(1)}, f32[2,384,128]{2,1,0:T(8,128)S(1)}, u32[]{:S(2)}, u32[]{:S(2)}) collective-permute-start(f32[2,384,128]{2,1,0:T(8,128)S(1)} %get-tuple-element.125), channel_id=1, source_target_pairs={{0,1},{2,3},{4,5},{6,7},{8,9},{10,11},{12,13},{14,15},{16,17},{18,... | collective-permute-start | bytes 1179656 | tf_op jit(solution)/shard_map/ppermute | solution.py:170
  23.4 9.2 %collective-permute-start.3 = (f32[2,384,128]{2,1,0:T(8,128)S(1)}, f32[2,384,128]{2,1,0:T(8,128)S(1)}, u32[]{:S(2)}, u32[]{:S(2)}) collective-permute-start(f32[2,384,128]{2,1,0:T(8,128)S(1)} %get-tuple-element.126), channel_id=1, source_target_pairs={{1,0},{3,2},{5,4},{7,6},{9,8},{11,10},{13,12},{15,14},{17,16},{19,... | collective-permute-start | bytes 1179656 | tf_op jit(solution)/shard_map/ppermute | solution.py:171
  53.4 10.8 %copy-start = (f32[12,2,128,128]{3,2,1,0:T(8,128)S(1)}, f32[12,2,128,128]{3,2,1,0:T(8,128)}, u32[]{:S(2)}) copy-start(f32[12,2,128,128]{3,2,1,0:T(8,128)} %probe_ref.1) | copy-start | bytes 4718596
  53.4 11.5 %copy-start.3 = (f32[26,128,128]{2,1,0:T(8,128)S(1)}, f32[26,128,128]{2,1,0:T(8,128)}, u32[]{:S(2)}) copy-start(f32[26,128,128]{2,1,0:T(8,128)} %get-tuple-element.116) | copy-start | bytes 5111812
  56.2 15.2 %collective-permute-start.4 = (f32[3,128,512]{2,1,0:T(8,128)}, f32[3,128,512]{2,1,0:T(8,128)S(1)}, u32[]{:S(2)}, u32[]{:S(2)}) collective-permute-start(f32[3,128,512]{2,1,0:T(8,128)} %get-tuple-element.122), channel_id=1, source_target_pairs={{0,2},{2,4},{4,6},{6,8},{8,10},{10,12},{12,14},{14,16},{16,18},{18... | collective-permute-start | bytes 2359304 | tf_op jit(solution)/shard_map/ppermute | solution.py:170
  62.2 13.9 %collective-permute-start.5 = (f32[3,128,512]{2,1,0:T(8,128)}, f32[3,128,512]{2,1,0:T(8,128)S(1)}, u32[]{:S(2)}, u32[]{:S(2)}) collective-permute-start(f32[3,128,512]{2,1,0:T(8,128)} %get-tuple-element.123), channel_id=1, source_target_pairs={{2,0},{4,2},{6,4},{8,6},{10,8},{12,10},{14,12},{16,14},{18,16},{20... | collective-permute-start | bytes 2359304 | tf_op jit(solution)/shard_map/ppermute | solution.py:171
  77.6 296.0 %collective-permute-start.7 = (f32[3,640,128]{2,1,0:T(8,128)}, f32[3,640,128]{2,1,0:T(8,128)}, u32[]{:S(2)}, u32[]{:S(2)}) collective-permute-start(f32[3,640,128]{2,1,0:T(8,128)} %get-tuple-element.120), channel_id=1, source_target_pairs={{1,0},{3,2},{5,4},{7,6},{9,8},{11,10},{13,12},{15,14},{17,16},{19,... | collective-permute-start | bytes 2949128 | tf_op jit(solution)/shard_map/ppermute | solution.py:171
  78.9 293.7 %collective-permute-start.6 = (f32[3,640,128]{2,1,0:T(8,128)}, f32[3,640,128]{2,1,0:T(8,128)}, u32[]{:S(2)}, u32[]{:S(2)}) collective-permute-start(f32[3,640,128]{2,1,0:T(8,128)} %get-tuple-element.121), channel_id=1, source_target_pairs={{0,1},{2,3},{4,5},{6,7},{8,9},{10,11},{12,13},{14,15},{16,17},{18,... | collective-permute-start | bytes 2949128 | tf_op jit(solution)/shard_map/ppermute | solution.py:170
  338.6 1.1 copy-start.1
  361.2 2.0 copy-start.5
  367.2 1.2 copy-start.6
  369.5 1.6 copy-start.2
  373.6 5.0 %copy-start.4 = (f32[2,128,256]{2,1,0:T(8,128)S(1)}, f32[2,128,256]{2,1,0:T(8,128)}, u32[]{:S(2)}) copy-start(f32[2,128,256]{2,1,0:T(8,128)} %param.30) | copy-start | bytes 786436
Sparse Core Ops, SparseCore 0:
  67.8 266.3 all-reduce.1

commit v2 on v1

--- a/solution.py
+++ b/solution.py
@@ -41,6 +41,10 @@
 
 def mm(a, b):
     return jnp.dot(a, b, preferred_element_type=jnp.float32)
+
+
+def place(channel, modes):
+    return channel + channel // modes
 
 
 def window_of(local_ref, position):
@@ -123,12 +127,13 @@
                 cr, ci = change[i * DET : i * DET + DET, :DET], change[i * DET : i * DET + DET, DET:]
                 pr, pi = probe_ref[k, 0], probe_ref[k, 1]
                 ar, ai = patch_ref[0], patch_ref[1]
-                sums_ref[2 * k] += ar * cr + ai * ci
-                sums_ref[2 * k + 1] += ar * ci - ai * cr
+                at = place(2 * k, modes)
+                sums_ref[at] += ar * cr + ai * ci
+                sums_ref[at + 1] += ar * ci - ai * cr
                 num_ref[0] += pr * cr + pi * ci
                 num_ref[1] += pr * ci - pi * cr
         ar, ai = patch_ref[0], patch_ref[1]
-        sums_ref[2 * modes] += ar * ar + ai * ai
+        sums_ref[modes] += ar * ar + ai * ai
         sums_ref[2 * modes + 1] += patterns_ref[position]
         for c in range(3):
             value = num_ref[c] if c < 2 else power
@@ -173,50 +178,277 @@
     return array
 
 
-def newton_steps(gram_re, gram_im):
-    mode_count = gram_re.shape[0]
-    upper = jnp.concatenate([gram_re, -gram_im], axis=1)
-    lower = jnp.concatenate([gram_im, gram_re], axis=1)
-    embedded = jnp.concatenate([upper, lower], axis=0)
-    frobenius = jnp.sqrt(jnp.sum(embedded * embedded))
-    identity = jnp.eye(2 * mode_count, dtype=jnp.float32)
+SPLITS = ((0, 6), (6, 13))
+AXES = ("x", "y")
+GRID = {"x": 4, "y": 4, "z": 8, "core": 2}
+
+
+def dot32(a, b, contract=(1, 0)):
+    return lax.dot_general(
+        a,
+        b,
+        (((contract[0],), (contract[1],)), ((), ())),
+        precision=highest,
+        preferred_element_type=jnp.float32,
+    )
+
+
+def my_place():
+    scan = lax.axis_index("scan")
+    tile = lax.axis_index("tile")
+    return {
+        "core": lax.rem(scan, 2),
+        "z": lax.rem(scan // 2, 8),
+        "x": lax.rem(scan // 16, 4),
+        "y": (scan // 64) * 2 + tile,
+    }
+
+
+def device_at(place_of):
+    high, low = place_of["y"] // 2, lax.rem(place_of["y"], 2)
+    return (((high * 4 + place_of["x"]) * 8 + place_of["z"]) * 2 + place_of["core"], low)
+
+
+def moved(here, axis, step):
+    return {**here, axis: lax.rem(here[axis] + step, GRID[axis])}
+
+
+def reduce_kernel(
+    sums_ref,
+    probe_ref,
+    upd_ref,
+    gram_ref,
+    held,
+    work,
+    first_a,
+    first_b,
+    second_a,
+    second_b,
+    part,
+    third,
+    both,
+    block,
+    grams,
+    send_sem,
+    recv_sem,
+):
+    here = my_place()
+    x, y, z, core = here["x"], here["y"], here["z"], here["core"]
+    partner = moved(here, "core", 1)
+    other = partner["core"]
+    peers = [moved(here, axis, step) for axis in ("x", "y", "z") for step in range(1, GRID[axis])]
+    barrier = pltpu.get_barrier_semaphore()
+    for peer in peers + [partner]:
+        pl.semaphore_signal(
+            barrier, inc=1, device_id=device_at(peer), device_id_type=pl.DeviceIdType.MESH
+        )
+    pl.semaphore_wait(barrier, len(peers) + 1)
+    started = []
+
+    def send(src, dst, peer):
+        index = len(started)
+        copy = pltpu.make_async_remote_copy(
+            src_ref=src,
+            dst_ref=dst,
+            send_sem=send_sem.at[index],
+            recv_sem=recv_sem.at[index],
+            device_id=device_at(peer),
+            device_id_type=pl.DeviceIdType.MESH,
+        )
+        copy.start()
+        started.append(copy)
+        return copy
+
+    def around(axis):
+        return [(step, moved(here, axis, step)) for step in range(1, GRID[axis])]
+
+    halves = []
+    for low, high in SPLITS:
+        rows = pl.ds(low, high - low)
+        halves.append(send(sums_ref.at[other, rows], held.at[rows], partner))
+    firsts = []
+    for half, (low, high) in enumerate(SPLITS):
+        halves[half].wait_recv()
+        rows = pl.ds(low, high - low)
+        work[rows] = sums_ref[core, rows] + held[rows]
+        if half == 0:
+            firsts.append(
+                [send(work.at[rows, p["x"]], first_a.at[i - 1], p) for i, p in around("x")]
+            )
+        else:
+            firsts.append(
+                [send(work.at[rows, :, p["y"]], first_b.at[i - 1], p) for i, p in around("y")]
+            )
+    seconds = []
+    rows_a, rows_b = (pl.ds(low, high - low) for low, high in SPLITS)
+    for copy in firsts[0]:
+        copy.wait_recv()
+    work[rows_a, x] += first_a[0] + first_a[1] + first_a[2]
+    seconds.append([send(work.at[rows_a, x, p["y"]], second_a.at[i - 1], p) for i, p in around("y")])
+    for copy in firsts[1]:
+        copy.wait_recv()
+    work[rows_b, :, y] += first_b[0] + first_b[1] + first_b[2]
+    seconds.append([send(work.at[rows_b, p["x"], y], second_b.at[i - 1], p) for i, p in around("x")])
+    for copy in seconds[0]:
+        copy.wait_recv()
+    part[rows_a] = work[rows_a, x, y] + second_a[0] + second_a[1] + second_a[2]
+    for copy in seconds[1]:
+        copy.wait_recv()
+    part[rows_b] = work[rows_b, x, y] + second_b[0] + second_b[1] + second_b[2]
+    part[pl.ds(13, 3)] = jnp.zeros((3, 8, DET), jnp.float32)
+
+    thirds = [
+        send(part.at[pl.ds(2 * p["z"], 2)], third.at[i - 1], p) for i, p in around("z")
+    ]
+    mine = part[pl.ds(2 * z, 2)]
+    for i, copy in enumerate(thirds):
+        copy.wait_recv()
+        mine = mine + third[i]
+    pair = pl.ds(2 * z, 2)
+    both[core, pair] = mine
+    backs = [send(both.at[core, pair], both.at[core, pair], p) for i, p in around("z")]
+    for copy in backs:
+        copy.wait_recv()
+    across = send(both.at[core], both.at[core], partner)
+    across.wait_recv()
+
+    light = both[0, 12]
+    power = jnp.zeros((8, DET), jnp.float32)
+    for channel in range(24):
+        old = probe_ref[channel, x, y]
+        power = power + old * old
+        new = old + both[channel // 12, channel % 12] / (light + PROBE_REG)
+        block[channel // 12, pl.ds(8 * (channel % 12), 8)] = new
+    for i in range(12):
+        upd_ref[core, i, x, y] = block[core, pl.ds(8 * i, 8)]
+    rows = jnp.concatenate(
+        [
+            jnp.concatenate([block[c, pl.ds(s, 12, stride=8)] for s in range(8)], axis=1)
+            for c in range(2)
+        ],
+        axis=0,
+    )
+    padded = jnp.concatenate([rows, jnp.zeros((DET - 24, 8 * DET), jnp.float32)], axis=0)
+    line = lax.broadcasted_iota(jnp.int32, (8, DET), 0)
+    total = jnp.sum(both[1, 12], axis=0, keepdims=True)
+    model = jnp.sum(power * light, axis=0, keepdims=True)
+    extra = jnp.where(line == 0, total, jnp.where(line == 1, model, 0.0))
+    grams[0, y] = jnp.concatenate([dot32(rows, padded, (1, 1)), extra], axis=0)
+
+    one_a, one_b = pl.ds(0, 6), pl.ds(6, 6)
+    gram_y = [send(grams.at[0, y], grams.at[0, y], p) for i, p in around("y")]
+    spot_a, spot_b = upd_ref.at[core, one_a, x, y], upd_ref.at[core, one_b, x, y]
+    near_a = [send(spot_a, spot_a, p) for i, p in around("y")]
+    near_b = [send(spot_b, spot_b, p) for i, p in around("x")]
+    for copy in gram_y:
+        copy.wait_recv()
+    grams[1, x] = (grams[0, 0] + grams[0, 1]) + (grams[0, 2] + grams[0, 3])
+    gram_x = [send(grams.at[1, x], grams.at[1, x], p) for i, p in around("x")]
+    for copy in near_a:
+        copy.wait_recv()
+    line_a = upd_ref.at[core, one_a, x]
+    far_a = [send(line_a, line_a, p) for i, p in around("x")]
+    for copy in near_b:
+        copy.wait_recv()
+    line_b = upd_ref.at[core, one_b, :, y]
+    far_b = [send(line_b, line_b, p) for i, p in around("y")]
+    last = [send(line_a, line_a, partner), send(line_b, line_b, partner)]
+    for copy in gram_x:
+        copy.wait_recv()
+    gram_ref[...] = (grams[1, 0] + grams[1, 1]) + (grams[1, 2] + grams[1, 3])
+    for step in range(1, 4):
+        far_a[step - 1].wait_recv()
+        got = upd_ref.at[core, one_a, lax.rem(x + 4 - step, 4)]
+        last.append(send(got, got, partner))
+        far_b[step - 1].wait_recv()
+        got = upd_ref.at[core, one_b, :, lax.rem(y + 4 - step, 4)]
+        last.append(send(got, got, partner))
+    for copy in last:
+        copy.wait_recv()
+    for copy in started:
+        copy.wait_send()
+
+
+COPIES = 55
+
+
+def reduced(sums, probe):
+    f32 = jnp.float32
+    return pl.pallas_call(
+        reduce_kernel,
+        out_shape=(
+            jax.ShapeDtypeStruct((2, 12, 4, 4, 8, DET), f32),
+            jax.ShapeDtypeStruct((32, DET), f32),
+        ),
+        in_specs=[VMEM, VMEM],
+        out_specs=(VMEM, VMEM),
+        scratch_shapes=[
+            pltpu.VMEM((13, 4, 4, 8, DET), f32),
+            pltpu.VMEM((13, 4, 4, 8, DET), f32),
+            pltpu.VMEM((3, 6, 4, 8, DET), f32),
+            pltpu.VMEM((3, 7, 4, 8, DET), f32),
+            pltpu.VMEM((3, 6, 8, DET), f32),
+            pltpu.VMEM((3, 7, 8, DET), f32),
+            pltpu.VMEM((16, 8, DET), f32),
+            pltpu.VMEM((7, 2, 8, DET), f32),
+            pltpu.VMEM((2, 16, 8, DET), f32),
+            pltpu.VMEM((2, 96, DET), f32),
+            pltpu.VMEM((2, 4, 32, DET), f32),
+            pltpu.SemaphoreType.DMA((COPIES,)),
+            pltpu.SemaphoreType.DMA((COPIES,)),
+        ],
+        compiler_params=pltpu.CompilerParams(collective_id=0, has_side_effects=True),
+        name="reduce_all",
+    )(sums.reshape(2, 13, 4, 4, 8, DET), probe.reshape(24, 4, 4, 8, DET))
+
+
+def mixing(gram):
+    size = 24
+    row = lax.broadcasted_iota(jnp.int32, (size, size), 0)
+    col = lax.broadcasted_iota(jnp.int32, (size, size), 1)
+    identity = jnp.where(row == col, 1.0, 0.0)
+    even = lax.rem(row, 2) == 0
+    turn = jnp.where(even & (col == row + 1), -1.0, jnp.where(~even & (col == row - 1), 1.0, 0.0))
+    products = gram[:size, :size]
+    embedded = products + dot32(dot32(turn, products), turn, (1, 1))
+    frobenius = jnp.sqrt(jnp.sum(embedded * embedded, keepdims=True))
     current = embedded / frobenius
     inverse = identity
     for repeat in range(NS_STEPS):
-        factor = 1.5 * identity - 0.5 * jnp.dot(
-            inverse, current, precision=highest, preferred_element_type=jnp.float32
-        )
-        current = jnp.dot(current, factor, precision=highest, preferred_element_type=jnp.float32)
-        inverse = jnp.dot(factor, inverse, precision=highest, preferred_element_type=jnp.float32)
-    inverse = inverse / jnp.sqrt(frobenius)
-    return (inverse[:mode_count, :mode_count], inverse[mode_count:, :mode_count])
-
-
-def gram_parts(mode_rows):
-    real_rows = mode_rows[0::2]
-    imag_rows = mode_rows[1::2]
-    gram_re = jnp.dot(
-        real_rows, real_rows.T, precision=highest, preferred_element_type=jnp.float32
-    ) + jnp.dot(imag_rows, imag_rows.T, precision=highest, preferred_element_type=jnp.float32)
-    gram_im = jnp.dot(
-        real_rows, imag_rows.T, precision=highest, preferred_element_type=jnp.float32
-    ) - jnp.dot(imag_rows, real_rows.T, precision=highest, preferred_element_type=jnp.float32)
-    return (gram_re, gram_im)
-
-
-def orthonormal_rows(mode_rows, gram_re, gram_im, power_ratio):
-    real_rows = mode_rows[0::2]
-    imag_rows = mode_rows[1::2]
-    mix_re, mix_im = newton_steps(gram_re, gram_im)
-    ortho_re = jnp.dot(
-        mix_re.T, real_rows, precision=highest, preferred_element_type=jnp.float32
-    ) - jnp.dot(mix_im.T, imag_rows, precision=highest, preferred_element_type=jnp.float32)
-    ortho_im = jnp.dot(
-        mix_im.T, real_rows, precision=highest, preferred_element_type=jnp.float32
-    ) + jnp.dot(mix_re.T, imag_rows, precision=highest, preferred_element_type=jnp.float32)
-    weight = jnp.sqrt(power_ratio * jnp.diagonal(gram_re))
-    joined = jnp.stack([ortho_re, ortho_im], axis=1) * weight[:, None, None]
-    return joined.reshape(mode_rows.shape)
+        factor = 1.5 * identity - 0.5 * dot32(inverse, current)
+        current = dot32(current, factor)
+        inverse = dot32(factor, inverse)
+    total = jnp.sum(gram[size : size + 1], keepdims=True)
+    model = jnp.sum(gram[size + 1 : size + 2], keepdims=True)
+    ratio = total / (model + TOTAL_EPS)
+    diagonal = jnp.sum(embedded * identity, axis=1, keepdims=True)
+    return inverse / jnp.sqrt(frobenius) * jnp.sqrt(ratio * diagonal)
+
+
+def ortho_kernel(gram_ref, upd_ref, out_ref):
+    mix = mixing(gram_ref[...])
+    tall = lax.broadcasted_iota(jnp.int32, (192, 24), 0)
+    wide = lax.broadcasted_iota(jnp.int32, (192, 24), 1)
+    expand = jnp.where(tall // 8 == wide, 1.0, 0.0)
+    large = dot32(dot32(expand, mix), expand, (1, 1))
+    row = lax.broadcasted_iota(jnp.int32, (192, 192), 0)
+    col = lax.broadcasted_iota(jnp.int32, (192, 192), 1)
+    large = jnp.where(lax.rem(row, 8) == lax.rem(col, 8), large, 0.0)
+    for b in range(0, 16, 2):
+        blocks = [upd_ref[:, b + i].reshape(192, DET) for i in range(2)]
+        result = dot32(large, jnp.concatenate(blocks, axis=1))
+        for i in range(2):
+            out_ref[:, b + i] = result[:, i * DET : i * DET + DET].reshape(24, 8, DET)
+
+
+def orthonormal(gram, updated):
+    return pl.pallas_call(
+        ortho_kernel,
+        out_shape=jax.ShapeDtypeStruct((24, 16, 8, DET), jnp.float32),
+        in_specs=[VMEM, VMEM],
+        out_specs=VMEM,
+        name="orthonormal",
+    )(gram, updated.reshape(24, 16, 8, DET))
 
 
 def fold_interior(frame_sum, folded, detector, block_rows, block_cols):
@@ -243,7 +475,6 @@
 
 
 def body(probe_modes, patterns, specimen, offsets):
-    mode_count = probe_modes.shape[0]
     block_rows, block_cols = specimen.shape[1:]
     sides = (("scan", 1), ("tile", 2))
     extended = extended_2(specimen, sides, DET)
@@ -257,14 +488,8 @@
     folded = extended_2(frame_sum, sides, DET)
     interior = fold_interior(frame_sum, folded, DET, block_rows, block_cols)
     new_specimen = specimen + interior[0:2] / (interior[2] + OBJECT_REG)[None]
-    totals = lax.psum(sums.reshape(2 * mode_count + 2, -1), ("scan", "tile"))
-    probe_rows = probe_modes.reshape(2 * mode_count, -1)
-    light = totals[2 * mode_count : 2 * mode_count + 1]
-    updated = probe_rows + totals[: 2 * mode_count] / (light + PROBE_REG)
-    power = jnp.sum(probe_rows * probe_rows, axis=0)
-    power_ratio = jnp.sum(totals[2 * mode_count + 1]) / (jnp.sum(power * light[0]) + TOTAL_EPS)
-    gram_re, gram_im = gram_parts(updated)
-    new_probe = orthonormal_rows(updated, gram_re, gram_im, power_ratio).reshape(probe_modes.shape)
+    updated, gram = reduced(sums, probe_modes)
+    new_probe = orthonormal(gram, updated).reshape(probe_modes.shape)
     return (new_probe, new_specimen)
 
 

time: 388 us -> 152 us (0.39)
  waiting for transfers between devices: 267 us -> 23.6 us
  Pallas kernels: 19.5 us -> 90.1 us
  local copies, waits for them, and re-layouts: 24 us -> 4.64 us
  matrix products: 15.9 us -> 0 us
  between operations: 16.5 us -> 0.83 us
  other arithmetic: 16.9 us -> 9.72 us
    psum x1 -> x0, waiting for transfers between devices: 248 us -> none  [body(): totals = lax.psum(sums.reshape(2 * mode_count + 2, -1), ('scan', 'tile'))]
    pallas_call x0 -> x2, Pallas kernels: none -> 70.7 us  [the longest x1 63.1 us: reduced(): pl.pallas_call(reduce_kernel, out_shape=(jax.ShapeDtypeStruct((2, 12, 4,...]
    dot_general x31 -> x0, matrix products: 15.9 us -> none  [the longest x1 2.28 us: orthonormal_rows(): jnp.dot(mix_re.T, imag_rows, precision=highest, preferred_element_type=jn...]
    slice x2 -> x0, local copies, waits for them, and re-layouts: 10.3 us -> none  [the longest x1 5.72 us: gram_parts(): real_rows = mode_rows[0::2]]
    unnamed x25 -> x13, local copies, waits for them, and re-layouts: 8.34 us -> 1.35 us
  transfers between devices with their start and end apart: 9 -> 8, of which waited for: 7 -> 6; matrix products, arithmetic and copies ran while one was open for 12% -> 3% of each run, Pallas kernels for 0% -> 47%
where the time goes in v2:
time: 152 us
  Pallas kernels  90.1 us (59%)
  waiting for transfers between devices  23.6 us (16%)
  starting transfers between devices  22.8 us (15%)
  other arithmetic  9.72 us (6%)
  local copies, waits for them, and re-layouts  4.64 us (3%)
    pallas_call x1, Pallas kernels, reduced(): pl.pallas_call(reduce_kernel, out_shape=(jax.ShapeDtypeStruct((2, 12, 4,...  63.1 us
    pallas_call x1, Pallas kernels, positions(): pl.pallas_call(positions_kernel, out_shape=(jax.ShapeDtypeStruct((2 * mod...  19.5 us
    ppermute x4, starting transfers between devices, extended_2(): before = lax.ppermute(last, axis, up)  16.4 us
    ppermute x4, waiting for transfers between devices, extended_2(): before = lax.ppermute(last, axis, up)  12.8 us
    ppermute x4, waiting for transfers between devices, extended_2(): after = lax.ppermute(first, axis, down)  10.8 us
    pallas_call x1, Pallas kernels, orthonormal(): pl.pallas_call(ortho_kernel, out_shape=jax.ShapeDtypeStruct((24, 16, 8, D...  7.6 us
    ppermute x4, starting transfers between devices, extended_2(): after = lax.ppermute(first, axis, down)  6.42 us
  transfers between devices with their start and end apart: 8, of which 6 were waited for; matrix products, arithmetic and copies ran while one was open for 3% of the time, Pallas kernels for 47%

profile of v2, /device:TPU:1, one launch (start us, length us, event | category | flops | bytes accessed | tf_op | source)
XLA Modules:
  0.0 151.8 jit_solution(2371643470889422357)
XLA Ops:
  0.6 4.9 %collective-permute-start = (f32[2,128,256]{2,1,0:T(8,128)}, f32[2,128,256]{2,1,0:T(8,128)S(1)}, u32[]{:S(2)}, u32[]{:S(2)}) collective-permute-start(f32[2,128,256]{2,1,0:T(8,128)} %param.30), channel_id=1, source_target_pairs={{0,2},{2,4},{4,6},{6,8},{8,10},{10,12},{12,14},{14,16},{16,18},{18... | collective-permute-start | bytes 786440 | tf_op jit(solution)/shard_map/ppermute | solution.py:175
  5.6 1.9 %collective-permute-start.1 = (f32[2,128,256]{2,1,0:T(8,128)}, f32[2,128,256]{2,1,0:T(8,128)S(1)}, u32[]{:S(2)}, u32[]{:S(2)}) collective-permute-start(f32[2,128,256]{2,1,0:T(8,128)} %param.30), channel_id=1, source_target_pairs={{2,0},{4,2},{6,4},{8,6},{10,8},{12,10},{14,12},{16,14},{18,16},{20... | collective-permute-start | bytes 786440 | tf_op jit(solution)/shard_map/ppermute | solution.py:176
  7.5 1.7 %collective-permute-done = f32[2,128,256]{2,1,0:T(8,128)S(1)} collective-permute-done((f32[2,128,256]{2,1,0:T(8,128)}, f32[2,128,256]{2,1,0:T(8,128)S(1)}, u32[]{:S(2)}, u32[]{:S(2)}) %collective-permute-start) | collective-permute-done | bytes 262176 | tf_op jit(solution)/shard_map/ppermute | solution.py:175
  9.2 1.0 constant_dynamic-update-slice_fusion.1
  10.2 3.3 %collective-permute-done.1 = f32[2,128,256]{2,1,0:T(8,128)S(1)} collective-permute-done((f32[2,128,256]{2,1,0:T(8,128)}, f32[2,128,256]{2,1,0:T(8,128)S(1)}, u32[]{:S(2)}, u32[]{:S(2)}) %collective-permute-start.1) | collective-permute-done | bytes 262176 | tf_op jit(solution)/shard_map/ppermute | solution.py:176
  13.6 3.2 %collective-permute-start.2 = (f32[2,384,128]{2,1,0:T(8,128)S(1)}, f32[2,384,128]{2,1,0:T(8,128)S(1)}, u32[]{:S(2)}, u32[]{:S(2)}) collective-permute-start(f32[2,384,128]{2,1,0:T(8,128)S(1)} %get-tuple-element.126), channel_id=1, source_target_pairs={{0,1},{2,3},{4,5},{6,7},{8,9},{10,11},{12,13},{14,15},{16,17},{18,... | collective-permute-start | bytes 1179656 | tf_op jit(solution)/shard_map/ppermute | solution.py:175
  16.8 1.3 collective-permute-start.3
  18.1 0.1 copy.10
  18.3 0.6 broadcast_subtract_fusion.local_ref
  18.9 4.1 %collective-permute-done.2 = f32[2,384,128]{2,1,0:T(8,128)S(1)} collective-permute-done((f32[2,384,128]{2,1,0:T(8,128)S(1)}, f32[2,384,128]{2,1,0:T(8,128)S(1)}, u32[]{:S(2)}, u32[]{:S(2)}) %collective-permute-start.2) | collective-permute-done | bytes 393248 | tf_op jit(solution)/shard_map/ppermute | solution.py:175
  23.0 3.0 %collective-permute-done.3 = f32[2,384,128]{2,1,0:T(8,128)S(1)} collective-permute-done((f32[2,384,128]{2,1,0:T(8,128)S(1)}, f32[2,384,128]{2,1,0:T(8,128)S(1)}, u32[]{:S(2)}, u32[]{:S(2)}) %collective-permute-start.3) | collective-permute-done | bytes 393248 | tf_op jit(solution)/shard_map/ppermute | solution.py:176
  26.0 1.3 pad_maximum_fusion.ext_ref
  27.3 19.5 %positions.1 = (f32[26,128,128]{2,1,0:T(8,128)}, f32[3,384,512]{2,1,0:T(8,128)}) custom-call(s32[4,2]{1,0:T(4,128)} %broadcast_subtract_fusion.local_ref, f32[12,2,128,128]{3,2,1,0:T(8,128)} %probe_ref.1, f32[4,128,128]{2,1,0:T(8,128)} %patterns_ref.1, f32[2,384,512]{2,1,0:T(8,128)} %pad_maximum_fusion.ext_ref, bf16[256,256]{1,0:T(8,128)(2,1)} %constant.225.clone.rh_ref, ...), custom_call_target="tpu_custom_call" | custom-call | tf_op jit(solution)/shard_map/positions/pallas_call | solution.py:151
  46.8 1.7 %fusion.9 = (f32[3,128,512]{2,1,0:T(8,128)S(1)}, f32[3,128,512]{2,1,0:T(8,128)S(1)}) fusion(f32[3,384,512]{2,1,0:T(8,128)} %get-tuple-element.121), kind=kLoop, calls=%fused_computation.28 | loop fusion | bytes 3145728 | tf_op jit(solution)/shard_map/slice | solution.py:173
  48.5 5.9 %collective-permute-start.4 = (f32[3,128,512]{2,1,0:T(8,128)S(1)}, f32[3,128,512]{2,1,0:T(8,128)S(1)}, u32[]{:S(2)}, u32[]{:S(2)}) collective-permute-start(f32[3,128,512]{2,1,0:T(8,128)S(1)} %get-tuple-element.124), channel_id=1, source_target_pairs={{0,2},{2,4},{4,6},{6,8},{8,10},{10,12},{12,14},{14,16},{16,18},{18... | collective-permute-start | bytes 2359304 | tf_op jit(solution)/shard_map/ppermute | solution.py:175
  54.4 1.9 %collective-permute-start.5 = (f32[3,128,512]{2,1,0:T(8,128)S(1)}, f32[3,128,512]{2,1,0:T(8,128)S(1)}, u32[]{:S(2)}, u32[]{:S(2)}) collective-permute-start(f32[3,128,512]{2,1,0:T(8,128)S(1)} %get-tuple-element.125), channel_id=1, source_target_pairs={{2,0},{4,2},{6,4},{8,6},{10,8},{12,10},{14,12},{16,14},{18,16},{20... | collective-permute-start | bytes 2359304 | tf_op jit(solution)/shard_map/ppermute | solution.py:176
  56.4 7.0 %collective-permute-done.4 = f32[3,128,512]{2,1,0:T(8,128)S(1)} collective-permute-done((f32[3,128,512]{2,1,0:T(8,128)S(1)}, f32[3,128,512]{2,1,0:T(8,128)S(1)}, u32[]{:S(2)}, u32[]{:S(2)}) %collective-permute-start.4) | collective-permute-done | bytes 786464 | tf_op jit(solution)/shard_map/ppermute | solution.py:175
  63.4 0.2 constant_dynamic-update-slice_fusion.4
  63.6 4.5 %collective-permute-done.5 = f32[3,128,512]{2,1,0:T(8,128)S(1)} collective-permute-done((f32[3,128,512]{2,1,0:T(8,128)S(1)}, f32[3,128,512]{2,1,0:T(8,128)S(1)}, u32[]{:S(2)}, u32[]{:S(2)}) %collective-permute-start.5) | collective-permute-done | bytes 786464 | tf_op jit(solution)/shard_map/ppermute | solution.py:176
  68.2 1.5 fusion.8
  69.7 2.3 %collective-permute-start.6 = (f32[3,640,128]{2,1,0:T(8,128)}, f32[3,640,128]{2,1,0:T(8,128)}, u32[]{:S(2)}, u32[]{:S(2)}) collective-permute-start(f32[3,640,128]{2,1,0:T(8,128)} %get-tuple-element.123), channel_id=1, source_target_pairs={{0,1},{2,3},{4,5},{6,7},{8,9},{10,11},{12,13},{14,15},{16,17},{18,... | collective-permute-start | bytes 2949128 | tf_op jit(solution)/shard_map/ppermute | solution.py:175
  72.0 1.3 collective-permute-start.7
  73.3 63.1 %reduce_all.1 = (f32[2,12,4,4,8,128]{5,4,3,2,1,0:T(8,128)}, f32[32,128]{1,0:T(8,128)}) custom-call(f32[2,13,4,4,8,128]{5,4,3,2,1,0:T(8,128)} %bitcast.9, f32[24,4,4,8,128]{4,3,2,1,0:T(8,128)} %bitcast.8), custom_call_target="tpu_custom_call" | custom-call | tf_op jit(solution)/shard_map/reduce_all/pallas_call | solution.py:377
  136.3 7.6 %orthonormal.1 = f32[24,16,8,128]{3,2,1,0:T(8,128)} custom-call(f32[32,128]{1,0:T(8,128)} %get-tuple-element.119.gram_ref, f32[24,16,8,128]{3,2,1,0:T(8,128)} %bitcast.11), custom_call_target="tpu_custom_call" | custom-call | tf_op jit(solution)/shard_map/orthonormal/pallas_call | solution.py:445
  143.9 1.1 slice_add_fusion
  145.1 1.0 fusion.6
  146.1 1.0 fusion.5
  147.0 1.0 fusion.4
  148.0 1.0 fusion.3
  149.0 1.0 fusion.2
  150.0 1.0 fusion.1
  151.0 0.7 fusion
  (17 shorter events, 0.3 us)
Async XLA Ops:
  0.6 17.5 %copy-start.3 = (s32[4,2]{0,1:T(2,128)S(1)}, s32[4,2]{0,1:T(2,128)}, u32[]{:S(2)}) copy-start(s32[4,2]{0,1:T(2,128)} %param.31) | copy-start | bytes 100
  0.6 8.5 %collective-permute-start = (f32[2,128,256]{2,1,0:T(8,128)}, f32[2,128,256]{2,1,0:T(8,128)S(1)}, u32[]{:S(2)}, u32[]{:S(2)}) collective-permute-start(f32[2,128,256]{2,1,0:T(8,128)} %param.30), channel_id=1, source_target_pairs={{0,2},{2,4},{4,6},{6,8},{8,10},{10,12},{12,14},{14,16},{16,18},{18... | collective-permute-start | bytes 786440 | tf_op jit(solution)/shard_map/ppermute | solution.py:175
  5.6 7.9 %collective-permute-start.1 = (f32[2,128,256]{2,1,0:T(8,128)}, f32[2,128,256]{2,1,0:T(8,128)S(1)}, u32[]{:S(2)}, u32[]{:S(2)}) collective-permute-start(f32[2,128,256]{2,1,0:T(8,128)} %param.30), channel_id=1, source_target_pairs={{2,0},{4,2},{6,4},{8,6},{10,8},{12,10},{14,12},{16,14},{18,16},{20... | collective-permute-start | bytes 786440 | tf_op jit(solution)/shard_map/ppermute | solution.py:176
  13.6 9.4 %collective-permute-start.2 = (f32[2,384,128]{2,1,0:T(8,128)S(1)}, f32[2,384,128]{2,1,0:T(8,128)S(1)}, u32[]{:S(2)}, u32[]{:S(2)}) collective-permute-start(f32[2,384,128]{2,1,0:T(8,128)S(1)} %get-tuple-element.126), channel_id=1, source_target_pairs={{0,1},{2,3},{4,5},{6,7},{8,9},{10,11},{12,13},{14,15},{16,17},{18,... | collective-permute-start | bytes 1179656 | tf_op jit(solution)/shard_map/ppermute | solution.py:175
  16.8 9.2 %collective-permute-start.3 = (f32[2,384,128]{2,1,0:T(8,128)S(1)}, f32[2,384,128]{2,1,0:T(8,128)S(1)}, u32[]{:S(2)}, u32[]{:S(2)}) collective-permute-start(f32[2,384,128]{2,1,0:T(8,128)S(1)} %get-tuple-element.127), channel_id=1, source_target_pairs={{1,0},{3,2},{5,4},{7,6},{9,8},{11,10},{13,12},{15,14},{17,16},{19,... | collective-permute-start | bytes 1179656 | tf_op jit(solution)/shard_map/ppermute | solution.py:176
  46.8 16.6 %copy-start = (f32[3,384,512]{2,1,0:T(8,128)S(1)}, f32[3,384,512]{2,1,0:T(8,128)}, u32[]{:S(2)}) copy-start(f32[3,384,512]{2,1,0:T(8,128)} %get-tuple-element.121) | copy-start | bytes 7077892
  48.5 14.9 %collective-permute-start.4 = (f32[3,128,512]{2,1,0:T(8,128)S(1)}, f32[3,128,512]{2,1,0:T(8,128)S(1)}, u32[]{:S(2)}, u32[]{:S(2)}) collective-permute-start(f32[3,128,512]{2,1,0:T(8,128)S(1)} %get-tuple-element.124), channel_id=1, source_target_pairs={{0,2},{2,4},{4,6},{6,8},{8,10},{10,12},{12,14},{14,16},{16,18},{18... | collective-permute-start | bytes 2359304 | tf_op jit(solution)/shard_map/ppermute | solution.py:175
  54.4 13.7 %collective-permute-start.5 = (f32[3,128,512]{2,1,0:T(8,128)S(1)}, f32[3,128,512]{2,1,0:T(8,128)S(1)}, u32[]{:S(2)}, u32[]{:S(2)}) collective-permute-start(f32[3,128,512]{2,1,0:T(8,128)S(1)} %get-tuple-element.125), channel_id=1, source_target_pairs={{2,0},{4,2},{6,4},{8,6},{10,8},{12,10},{14,12},{16,14},{18,16},{20... | collective-permute-start | bytes 2359304 | tf_op jit(solution)/shard_map/ppermute | solution.py:176
  68.1 1.6 %copy-start.1 = (f32[3,128,512]{2,1,0:T(8,128)}, f32[3,128,512]{2,1,0:T(8,128)S(1)}, u32[]{:S(2)}) copy-start(f32[3,128,512]{2,1,0:T(8,128)S(1)} %collective-permute-done.5) | copy-start | bytes 2359300
  69.7 75.4 %collective-permute-start.6 = (f32[3,640,128]{2,1,0:T(8,128)}, f32[3,640,128]{2,1,0:T(8,128)}, u32[]{:S(2)}, u32[]{:S(2)}) collective-permute-start(f32[3,640,128]{2,1,0:T(8,128)} %get-tuple-element.123), channel_id=1, source_target_pairs={{0,1},{2,3},{4,5},{6,7},{8,9},{10,11},{12,13},{14,15},{16,17},{18,... | collective-permute-start | bytes 2949128 | tf_op jit(solution)/shard_map/ppermute | solution.py:175
  72.0 74.1 %collective-permute-start.7 = (f32[3,640,128]{2,1,0:T(8,128)}, f32[3,640,128]{2,1,0:T(8,128)}, u32[]{:S(2)}, u32[]{:S(2)}) collective-permute-start(f32[3,640,128]{2,1,0:T(8,128)} %get-tuple-element.122), channel_id=1, source_target_pairs={{1,0},{3,2},{5,4},{7,6},{9,8},{11,10},{13,12},{15,14},{17,16},{19,... | collective-permute-start | bytes 2949128 | tf_op jit(solution)/shard_map/ppermute | solution.py:176
  143.9 7.1 %copy-start.2 = (f32[2,128,256]{2,1,0:T(8,128)S(1)}, f32[2,128,256]{2,1,0:T(8,128)}, u32[]{:S(2)}) copy-start(f32[2,128,256]{2,1,0:T(8,128)} %param.30) | copy-start | bytes 786436

commit v3 on v2

--- a/solution.py
+++ b/solution.py
@@ -48,8 +48,8 @@
 
 
 def window_of(local_ref, position):
-    row = local_ref[position, 0]
-    col = local_ref[position, 1]
+    row = local_ref[position, 0] - (lax.axis_index("scan") - 1) * DET
+    col = local_ref[position, 1] - (2 * lax.axis_index("tile") - 1) * DET
     tile = jnp.minimum(col // DET, 2)
     slab = jnp.minimum(row // 8, 31)
     return pl.multiple_of(slab * 8, 8), row - slab * 8, pl.multiple_of(tile * DET, DET), col - tile * DET
@@ -165,17 +165,89 @@
     )(local, probe, patterns, extended, *split_tables())
 
 
-def extended_2(array, sides, width):
-    for axis, dim in sides:
-        size, length = (lax.axis_size(axis), array.shape[dim])
-        up = [(i, (i + 1) % size) for i in range(size - 1)]
-        down = [(j, i) for i, j in up]
-        last = lax.slice_in_dim(array, length - width, length, axis=dim)
-        first = lax.slice_in_dim(array, 0, width, axis=dim)
-        before = lax.ppermute(last, axis, up)
-        after = lax.ppermute(first, axis, down)
-        array = jnp.concatenate([before, array, after], axis=dim)
-    return array
+def signal_all(peers):
+    barrier = pltpu.get_barrier_semaphore()
+    for peer in peers:
+        pl.semaphore_signal(barrier, inc=1, device_id=peer, device_id_type=pl.DeviceIdType.MESH)
+    pl.semaphore_wait(barrier, len(peers))
+
+
+class Copies:
+    def __init__(self, send_sem, recv_sem):
+        self.send_sem, self.recv_sem, self.started = send_sem, recv_sem, []
+
+    def send(self, src, dst, device):
+        index = len(self.started)
+        copy = pltpu.make_async_remote_copy(
+            src_ref=src,
+            dst_ref=dst,
+            send_sem=self.send_sem.at[index],
+            recv_sem=self.recv_sem.at[index],
+            device_id=device,
+            device_id_type=pl.DeviceIdType.MESH,
+        )
+        copy.start()
+        self.started.append(copy)
+        return copy
+
+    def finish(self):
+        for copy in self.started:
+            copy.wait_send()
+
+
+def neighbours():
+    scan, tile = lax.axis_index("scan"), lax.axis_index("tile")
+    size = lax.axis_size("scan")
+    up = (lax.rem(scan + size - 1, size), tile)
+    down = (lax.rem(scan + 1, size), tile)
+    return up, down, (scan, 1 - tile)
+
+
+def halo_kernel(spec_ref, ext_ref, send_sem, recv_sem):
+    scan, tile = lax.axis_index("scan"), lax.axis_index("tile")
+    up, down, across = neighbours()
+    signal_all([up, down, across])
+    copies = Copies(send_sem, recv_sem)
+    own, above, below = pl.ds(DET, DET), pl.ds(0, DET), pl.ds(2 * DET, DET)
+    middle = pl.ds(DET, 2 * DET)
+    given = pl.ds(pl.multiple_of((1 - tile) * DET, DET), DET)
+    empty = pl.ds(pl.multiple_of(tile * 3 * DET, DET), DET)
+    filled = pl.ds(pl.multiple_of((1 - tile) * 3 * DET, DET), DET)
+    side = copies.send(spec_ref.at[:, :, given], ext_ref.at[:, own, empty], across)
+    rest = [
+        copies.send(spec_ref, ext_ref.at[:, below, middle], up),
+        copies.send(spec_ref, ext_ref.at[:, above, middle], down),
+    ]
+    ext_ref[:, own, middle] = spec_ref[...]
+    ext_ref[:, :, empty] = jnp.zeros((2, 3 * DET, DET), jnp.float32)
+    side.wait_recv()
+    corner = ext_ref.at[:, own, filled]
+    rest.append(copies.send(corner, ext_ref.at[:, below, filled], up))
+    rest.append(copies.send(corner, ext_ref.at[:, above, filled], down))
+    for copy in rest:
+        copy.wait_recv()
+
+    @pl.when(scan == 0)
+    def _():
+        ext_ref[:, above] = jnp.zeros((2, DET, 4 * DET), jnp.float32)
+
+    @pl.when(scan == lax.axis_size("scan") - 1)
+    def _():
+        ext_ref[:, below] = jnp.zeros((2, DET, 4 * DET), jnp.float32)
+
+    copies.finish()
+
+
+def extended_of(specimen):
+    return pl.pallas_call(
+        halo_kernel,
+        out_shape=jax.ShapeDtypeStruct((2, 3 * DET, 4 * DET), jnp.float32),
+        in_specs=[VMEM],
+        out_specs=VMEM,
+        scratch_shapes=[pltpu.SemaphoreType.DMA((5,)), pltpu.SemaphoreType.DMA((5,))],
+        compiler_params=pltpu.CompilerParams(collective_id=1, has_side_effects=True),
+        name="halo",
+    )(specimen)
 
 
 SPLITS = ((0, 6), (6, 13))
@@ -216,8 +288,11 @@
 def reduce_kernel(
     sums_ref,
     probe_ref,
+    frame_ref,
+    spec_ref,
     upd_ref,
-    gram_ref,
+    mix_ref,
+    new_ref,
     held,
     work,
     first_a,
@@ -229,6 +304,9 @@
     both,
     block,
     grams,
+    rows_in,
+    frame,
+    cols_in,
     send_sem,
     recv_sem,
 ):
@@ -236,28 +314,14 @@
     x, y, z, core = here["x"], here["y"], here["z"], here["core"]
     partner = moved(here, "core", 1)
     other = partner["core"]
+    scan, tile = lax.axis_index("scan"), lax.axis_index("tile")
+    up, down, across_tile = neighbours()
     peers = [moved(here, axis, step) for axis in ("x", "y", "z") for step in range(1, GRID[axis])]
-    barrier = pltpu.get_barrier_semaphore()
-    for peer in peers + [partner]:
-        pl.semaphore_signal(
-            barrier, inc=1, device_id=device_at(peer), device_id_type=pl.DeviceIdType.MESH
-        )
-    pl.semaphore_wait(barrier, len(peers) + 1)
-    started = []
+    signal_all([device_at(peer) for peer in peers + [partner]] + [up, down])
+    copies = Copies(send_sem, recv_sem)
 
     def send(src, dst, peer):
-        index = len(started)
-        copy = pltpu.make_async_remote_copy(
-            src_ref=src,
-            dst_ref=dst,
-            send_sem=send_sem.at[index],
-            recv_sem=recv_sem.at[index],
-            device_id=device_at(peer),
-            device_id_type=pl.DeviceIdType.MESH,
-        )
-        copy.start()
-        started.append(copy)
-        return copy
+        return copies.send(src, dst, device_at(peer))
 
     def around(axis):
         return [(step, moved(here, axis, step)) for step in range(1, GRID[axis])]
@@ -266,6 +330,9 @@
     for low, high in SPLITS:
         rows = pl.ds(low, high - low)
         halves.append(send(sums_ref.at[other, rows], held.at[rows], partner))
+    span = pl.ds(pl.multiple_of((1 - tile) * DET, DET), 3 * DET)
+    from_below = copies.send(frame_ref.at[:, pl.ds(0, DET), span], rows_in.at[0], up)
+    from_above = copies.send(frame_ref.at[:, pl.ds(2 * DET, DET), span], rows_in.at[1], down)
     firsts = []
     for half, (low, high) in enumerate(SPLITS):
         halves[half].wait_recv()
@@ -300,6 +367,15 @@
     thirds = [
         send(part.at[pl.ds(2 * p["z"], 2)], third.at[i - 1], p) for i, p in around("z")
     ]
+    from_below.wait_recv()
+    from_above.wait_recv()
+    last_row = lax.axis_size("scan") - 1
+    for c in range(3):
+        added = jnp.where(scan == last_row, 0.0, rows_in[0, c])
+        added = added + jnp.where(scan == 0, 0.0, rows_in[1, c])
+        frame[c] = frame_ref[c, pl.ds(DET, DET), span] + added
+    beyond = pl.ds(pl.multiple_of((1 - tile) * 2 * DET, DET), DET)
+    sides = copies.send(frame.at[:, :, beyond], cols_in, across_tile)
     mine = part[pl.ds(2 * z, 2)]
     for i, copy in enumerate(thirds):
         copy.wait_recv()
@@ -355,7 +431,15 @@
     last = [send(line_a, line_a, partner), send(line_b, line_b, partner)]
     for copy in gram_x:
         copy.wait_recv()
-    gram_ref[...] = (grams[1, 0] + grams[1, 1]) + (grams[1, 2] + grams[1, 3])
+    mix_ref[...] = expanded(mixing((grams[1, 0] + grams[1, 1]) + (grams[1, 2] + grams[1, 3])))
+    sides.wait_recv()
+    inside = [frame[c, :, pl.ds(pl.multiple_of(tile * DET, DET), 2 * DET)] for c in range(3)]
+    for c in range(3):
+        left = jnp.where(tile == 1, cols_in[c], 0.0)
+        right = jnp.where(tile == 0, cols_in[c], 0.0)
+        inside[c] = inside[c] + jnp.concatenate([left, right], axis=1)
+    for c in range(2):
+        new_ref[c] = spec_ref[c] + inside[c] / (inside[2] + OBJECT_REG)
     for step in range(1, 4):
         far_a[step - 1].wait_recv()
         got = upd_ref.at[core, one_a, lax.rem(x + 4 - step, 4)]
@@ -365,23 +449,23 @@
         last.append(send(got, got, partner))
     for copy in last:
         copy.wait_recv()
-    for copy in started:
-        copy.wait_send()
-
-
-COPIES = 55
-
-
-def reduced(sums, probe):
+    copies.finish()
+
+
+COPIES = 58
+
+
+def reduced(sums, probe, frame, specimen):
     f32 = jnp.float32
     return pl.pallas_call(
         reduce_kernel,
         out_shape=(
             jax.ShapeDtypeStruct((2, 12, 4, 4, 8, DET), f32),
-            jax.ShapeDtypeStruct((32, DET), f32),
+            jax.ShapeDtypeStruct((192, 192), f32),
+            jax.ShapeDtypeStruct(specimen.shape, f32),
         ),
-        in_specs=[VMEM, VMEM],
-        out_specs=(VMEM, VMEM),
+        in_specs=[VMEM] * 4,
+        out_specs=(VMEM,) * 3,
         scratch_shapes=[
             pltpu.VMEM((13, 4, 4, 8, DET), f32),
             pltpu.VMEM((13, 4, 4, 8, DET), f32),
@@ -394,12 +478,15 @@
             pltpu.VMEM((2, 16, 8, DET), f32),
             pltpu.VMEM((2, 96, DET), f32),
             pltpu.VMEM((2, 4, 32, DET), f32),
+            pltpu.VMEM((2, 3, DET, 3 * DET), f32),
+            pltpu.VMEM((3, DET, 3 * DET), f32),
+            pltpu.VMEM((3, DET, DET), f32),
             pltpu.SemaphoreType.DMA((COPIES,)),
             pltpu.SemaphoreType.DMA((COPIES,)),
         ],
         compiler_params=pltpu.CompilerParams(collective_id=0, has_side_effects=True),
         name="reduce_all",
-    )(sums.reshape(2, 13, 4, 4, 8, DET), probe.reshape(24, 4, 4, 8, DET))
+    )(sums.reshape(2, 13, 4, 4, 8, DET), probe.reshape(24, 4, 4, 8, DET), frame, specimen)
 
 
 def mixing(gram):
@@ -425,15 +512,18 @@
     return inverse / jnp.sqrt(frobenius) * jnp.sqrt(ratio * diagonal)
 
 
-def ortho_kernel(gram_ref, upd_ref, out_ref):
-    mix = mixing(gram_ref[...])
+def expanded(mix):
     tall = lax.broadcasted_iota(jnp.int32, (192, 24), 0)
     wide = lax.broadcasted_iota(jnp.int32, (192, 24), 1)
     expand = jnp.where(tall // 8 == wide, 1.0, 0.0)
     large = dot32(dot32(expand, mix), expand, (1, 1))
     row = lax.broadcasted_iota(jnp.int32, (192, 192), 0)
     col = lax.broadcasted_iota(jnp.int32, (192, 192), 1)
-    large = jnp.where(lax.rem(row, 8) == lax.rem(col, 8), large, 0.0)
+    return jnp.where(lax.rem(row, 8) == lax.rem(col, 8), large, 0.0)
+
+
+def ortho_kernel(mix_ref, upd_ref, out_ref):
+    large = mix_ref[...]
     for b in range(0, 16, 2):
         blocks = [upd_ref[:, b + i].reshape(192, DET) for i in range(2)]
         result = dot32(large, jnp.concatenate(blocks, axis=1))
@@ -441,55 +531,21 @@
             out_ref[:, b + i] = result[:, i * DET : i * DET + DET].reshape(24, 8, DET)
 
 
-def orthonormal(gram, updated):
+def orthonormal(mix, updated):
     return pl.pallas_call(
         ortho_kernel,
         out_shape=jax.ShapeDtypeStruct((24, 16, 8, DET), jnp.float32),
         in_specs=[VMEM, VMEM],
         out_specs=VMEM,
         name="orthonormal",
-    )(gram, updated.reshape(24, 16, 8, DET))
-
-
-def fold_interior(frame_sum, folded, detector, block_rows, block_cols):
-    rows_end = block_rows + 3 * detector
-    cols_end = block_cols + 3 * detector
-    centre_rows = slice(2 * detector, 2 * detector + block_rows)
-    centre_cols = slice(2 * detector, 2 * detector + block_cols)
-    interior = frame_sum[:, detector : detector + block_rows, detector : detector + block_cols]
-    interior = interior.at[:, :detector, :].add(folded[:, :detector, centre_cols])
-    interior = interior.at[:, block_rows - detector :, :].add(folded[:, rows_end:, centre_cols])
-    interior = interior.at[:, :, :detector].add(folded[:, centre_rows, :detector])
-    interior = interior.at[:, :, block_cols - detector :].add(folded[:, centre_rows, cols_end:])
-    interior = interior.at[:, :detector, :detector].add(folded[:, :detector, :detector])
-    interior = interior.at[:, :detector, block_cols - detector :].add(
-        folded[:, :detector, cols_end:]
-    )
-    interior = interior.at[:, block_rows - detector :, :detector].add(
-        folded[:, rows_end:, :detector]
-    )
-    interior = interior.at[:, block_rows - detector :, block_cols - detector :].add(
-        folded[:, rows_end:, cols_end:]
-    )
-    return interior
+    )(mix, updated.reshape(24, 16, 8, DET))
 
 
 def body(probe_modes, patterns, specimen, offsets):
-    block_rows, block_cols = specimen.shape[1:]
-    sides = (("scan", 1), ("tile", 2))
-    extended = extended_2(specimen, sides, DET)
-    base = jnp.stack(
-        [
-            lax.axis_index("scan") * block_rows - DET,
-            lax.axis_index("tile") * block_cols - DET,
-        ]
-    )
-    sums, frame_sum = positions(offsets - base, probe_modes, patterns, extended)
-    folded = extended_2(frame_sum, sides, DET)
-    interior = fold_interior(frame_sum, folded, DET, block_rows, block_cols)
-    new_specimen = specimen + interior[0:2] / (interior[2] + OBJECT_REG)[None]
-    updated, gram = reduced(sums, probe_modes)
-    new_probe = orthonormal(gram, updated).reshape(probe_modes.shape)
+    extended = extended_of(specimen)
+    sums, frame = positions(offsets, probe_modes, patterns, extended)
+    updated, mix, new_specimen = reduced(sums, probe_modes, frame, specimen)
+    new_probe = orthonormal(mix, updated).reshape(probe_modes.shape)
     return (new_probe, new_specimen)
 
 

time: 152 us -> 104 us (0.68)
  waiting for transfers between devices: 23.6 us -> 0 us
  starting transfers between devices: 22.8 us -> 0 us
  Pallas kernels: 90.1 us -> 101 us
  other arithmetic: 9.72 us -> 0 us
  local copies, waits for them, and re-layouts: 4.64 us -> 2.04 us
    ppermute x8 -> x0, waiting for transfers between devices: 23.6 us -> none  [the longest x4 12.8 us: extended_2(): before = lax.ppermute(last, axis, up)]
    ppermute x8 -> x0, starting transfers between devices: 22.8 us -> none  [the longest x4 16.4 us: extended_2(): before = lax.ppermute(last, axis, up)]
    pallas_call x0 -> x1, Pallas kernels: none -> 20.6 us  [extended_of(): pl.pallas_call(halo_kernel, out_shape=jax.ShapeDtypeStruct((2, 3 * DET, 4...]
    pallas_call x1, Pallas kernels: 63.1 us -> 56.5 us  [reduced(): pl.pallas_call(reduce_kernel, out_shape=(jax.ShapeDtypeStruct((2, 12, 4,...]
    scatter-add x6 -> x0, other arithmetic: 5.87 us -> none  [the longest x1 0.98 us: fold_interior(): interior.at[:, block_rows - detector:, :detector]]
    pallas_call x1, Pallas kernels: 7.6 us -> 4.12 us  [orthonormal(): pl.pallas_call(ortho_kernel, out_shape=jax.ShapeDtypeStruct((24, 16, 8, D...]
    slice x3 -> x0, local copies, waits for them, and re-layouts: 3.21 us -> none  [the longest x2 1.71 us: extended_2(): last = lax.slice_in_dim(array, length - width, length, axis=dim)]
    add x2 -> x0, other arithmetic: 1.87 us -> none  [the longest x1 1.13 us: fold_interior(): interior.at[:, block_rows - detector:, :]]
  transfers between devices with their start and end apart: 8 -> 0, of which waited for: 6 -> 0; matrix products, arithmetic and copies ran while one was open for 3% -> 0% of each run, Pallas kernels for 47% -> 0%
where the time goes in v3:
time: 104 us; the launch traced here: 103 us
  Pallas kernels  101 us (97%)
  local copies, waits for them, and re-layouts  2.04 us (2%)
    pallas_call x1, Pallas kernels, reduced(): pl.pallas_call(reduce_kernel, out_shape=(jax.ShapeDtypeStruct((2, 12, 4,...  56.5 us
    pallas_call x1, Pallas kernels, extended_of(): pl.pallas_call(halo_kernel, out_shape=jax.ShapeDtypeStruct((2, 3 * DET, 4...  20.6 us
    pallas_call x1, Pallas kernels, positions(): pl.pallas_call(positions_kernel, out_shape=(jax.ShapeDtypeStruct((2 * mod...  19.5 us
    pallas_call x1, Pallas kernels, orthonormal(): pl.pallas_call(ortho_kernel, out_shape=jax.ShapeDtypeStruct((24, 16, 8, D...  4.12 us

profile of v3, /device:TPU:1, one launch (start us, length us, event | category | flops | bytes accessed | tf_op | source)
XLA Modules:
  0.0 103.4 jit_solution(14807076876264259256)
XLA Ops:
  0.6 1.3 %copy.10.local_ref = s32[4,2]{1,0:T(4,128)} copy(s32[4,2]{0,1:T(2,128)} %param.11) | data formatting | bytes 64 | tf_op args[3]
  2.0 20.6 %halo.1.ext_ref = f32[2,384,512]{2,1,0:T(8,128)} custom-call(f32[2,128,256]{2,1,0:T(8,128)} %spec_ref.3), custom_call_target="tpu_custom_call" | custom-call | tf_op jit(solution)/shard_map/halo/pallas_call | solution.py:242
  22.6 19.5 %positions.1 = (f32[26,128,128]{2,1,0:T(8,128)}, f32[3,384,512]{2,1,0:T(8,128)}) custom-call(s32[4,2]{1,0:T(4,128)} %copy.10.local_ref, f32[12,2,128,128]{3,2,1,0:T(8,128)} %probe_ref.1, f32[4,128,128]{2,1,0:T(8,128)} %patterns_ref.1, f32[2,384,512]{2,1,0:T(8,128)} %halo.1.ext_ref, bf16[256,256]{1,0:T(8,128)(2,1)} %constant.8.clone.rh_ref, ...), custom_call_target="tpu_custom_call" | custom-call | tf_op jit(solution)/shard_map/positions/pallas_call | solution.py:151
  42.1 56.5 %reduce_all.1 = (f32[2,12,4,4,8,128]{5,4,3,2,1,0:T(8,128)}, f32[192,192]{1,0:T(8,128)}, f32[2,128,256]{2,1,0:T(8,128)}) custom-call(f32[2,13,4,4,8,128]{5,4,3,2,1,0:T(8,128)} %bitcast.5, f32[24,4,4,8,128]{4,3,2,1,0:T(8,128)} %bitcast.4, f32[3,384,512]{2,1,0:T(8,128)} %get-tuple-element.8.frame_ref, f32[2,128,256]{2,1,0:T(8,128)} %spec_ref.3), custom_call_target="tpu_custom_call" | custom-call | tf_op jit(solution)/shard_map/reduce_all/pallas_call | solution.py:460
  98.5 0.0 copy-start
  98.5 4.1 %orthonormal.1 = f32[24,16,8,128]{3,2,1,0:T(8,128)} custom-call(f32[192,192]{1,0:T(8,128)} %get-tuple-element.9.mix_ref, f32[24,16,8,128]{3,2,1,0:T(8,128)} %bitcast.7), custom_call_target="tpu_custom_call" | custom-call | tf_op jit(solution)/shard_map/orthonormal/pallas_call | solution.py:535
  102.7 0.0 copy-done
  102.7 0.7 copy.12
Async XLA Ops:
  98.5 4.1 %copy-start = (f32[2,128,256]{2,1,0:T(8,128)S(1)}, f32[2,128,256]{2,1,0:T(8,128)}, u32[]{:S(2)}) copy-start(f32[2,128,256]{2,1,0:T(8,128)} %get-tuple-element.15) | copy-start | bytes 786436

commit v4 on v3

--- a/solution.py
+++ b/solution.py
@@ -12,6 +12,7 @@
 NS_STEPS = 8
 DET = 128
 TALL = 136
+LIMIT = 20 * 2**20
 LIGHT_FLOOR = 0.05
 OBJECT_REG = 0.5
 PROBE_REG = 1.0
@@ -31,7 +32,7 @@
         high = matrix.astype(ml_dtypes.bfloat16)
         low = (matrix - high.astype(np.float64)).astype(ml_dtypes.bfloat16)
         tables += [high, low]
-    return [jnp.asarray(table) for table in tables]
+    return jnp.asarray(np.stack(tables))
 
 
 def split(value):
@@ -60,10 +61,7 @@
     probe_ref,
     patterns_ref,
     ext_ref,
-    rh_ref,
-    rl_ref,
-    lh_ref,
-    ll_ref,
+    tables_ref,
     sums_ref,
     frame_ref,
     patch_ref,
@@ -72,6 +70,7 @@
 ):
     modes = probe_ref.shape[0]
     pairs = modes // 2
+    rh_ref, rl_ref, lh_ref, ll_ref = (tables_ref.at[i] for i in range(4))
     power = jnp.zeros((DET, DET), jnp.float32)
     for k in range(modes):
         power = power + probe_ref[k, 0] * probe_ref[k, 0] + probe_ref[k, 1] * probe_ref[k, 1]
@@ -154,15 +153,16 @@
             jax.ShapeDtypeStruct((2 * modes + 2, DET, DET), jnp.float32),
             jax.ShapeDtypeStruct((3,) + extended.shape[1:], jnp.float32),
         ),
-        in_specs=[SMEM] + [VMEM] * 7,
+        in_specs=[SMEM] + [VMEM] * 4,
         out_specs=(VMEM, VMEM),
         scratch_shapes=[
             pltpu.VMEM((2, DET, DET), jnp.float32),
             pltpu.VMEM((modes // 2, 2 * DET, 2 * DET), jnp.float32),
             pltpu.VMEM((2, DET, DET), jnp.float32),
         ],
+        compiler_params=pltpu.CompilerParams(vmem_limit_bytes=LIMIT),
         name="positions",
-    )(local, probe, patterns, extended, *split_tables())
+    )(local, probe, patterns, extended, split_tables())
 
 
 def signal_all(peers):
@@ -213,17 +213,24 @@
     given = pl.ds(pl.multiple_of((1 - tile) * DET, DET), DET)
     empty = pl.ds(pl.multiple_of(tile * 3 * DET, DET), DET)
     filled = pl.ds(pl.multiple_of((1 - tile) * 3 * DET, DET), DET)
-    side = copies.send(spec_ref.at[:, :, given], ext_ref.at[:, own, empty], across)
+    pieces = [(c, r * 64) for c in range(2) for r in range(2)]
+    side = [
+        copies.send(
+            spec_ref.at[c, pl.ds(r, 64), given], ext_ref.at[c, pl.ds(DET + r, 64), empty], across
+        )
+        for c, r in pieces
+    ]
     rest = [
         copies.send(spec_ref, ext_ref.at[:, below, middle], up),
         copies.send(spec_ref, ext_ref.at[:, above, middle], down),
     ]
     ext_ref[:, own, middle] = spec_ref[...]
     ext_ref[:, :, empty] = jnp.zeros((2, 3 * DET, DET), jnp.float32)
-    side.wait_recv()
-    corner = ext_ref.at[:, own, filled]
-    rest.append(copies.send(corner, ext_ref.at[:, below, filled], up))
-    rest.append(copies.send(corner, ext_ref.at[:, above, filled], down))
+    for (c, r), copy in zip(pieces, side):
+        copy.wait_recv()
+        corner = ext_ref.at[c, pl.ds(DET + r, 64), filled]
+        rest.append(copies.send(corner, ext_ref.at[c, pl.ds(2 * DET + r, 64), filled], up))
+        rest.append(copies.send(corner, ext_ref.at[c, pl.ds(r, 64), filled], down))
     for copy in rest:
         copy.wait_recv()
 
@@ -244,8 +251,8 @@
         out_shape=jax.ShapeDtypeStruct((2, 3 * DET, 4 * DET), jnp.float32),
         in_specs=[VMEM],
         out_specs=VMEM,
-        scratch_shapes=[pltpu.SemaphoreType.DMA((5,)), pltpu.SemaphoreType.DMA((5,))],
-        compiler_params=pltpu.CompilerParams(collective_id=1, has_side_effects=True),
+        scratch_shapes=[pltpu.SemaphoreType.DMA((14,)), pltpu.SemaphoreType.DMA((14,))],
+        compiler_params=pltpu.CompilerParams(collective_id=1, has_side_effects=True, vmem_limit_bytes=LIMIT),
         name="halo",
     )(specimen)
 
@@ -484,7 +491,7 @@
             pltpu.SemaphoreType.DMA((COPIES,)),
             pltpu.SemaphoreType.DMA((COPIES,)),
         ],
-        compiler_params=pltpu.CompilerParams(collective_id=0, has_side_effects=True),
+        compiler_params=pltpu.CompilerParams(collective_id=0, has_side_effects=True, vmem_limit_bytes=LIMIT),
         name="reduce_all",
     )(sums.reshape(2, 13, 4, 4, 8, DET), probe.reshape(24, 4, 4, 8, DET), frame, specimen)
 
@@ -537,6 +544,7 @@
         out_shape=jax.ShapeDtypeStruct((24, 16, 8, DET), jnp.float32),
         in_specs=[VMEM, VMEM],
         out_specs=VMEM,
+        compiler_params=pltpu.CompilerParams(vmem_limit_bytes=LIMIT),
         name="orthonormal",
     )(mix, updated.reshape(24, 16, 8, DET))
 

time: 104 us -> 94.6 us (0.910)
  Pallas kernels: 101 us -> 90.2 us
  local copies, waits for them, and re-layouts: 2.04 us -> 3.58 us
    pallas_call x1, Pallas kernels: 56.5 us -> 52.3 us  [reduced(): pl.pallas_call(reduce_kernel, out_shape=(jax.ShapeDtypeStruct((2, 12, 4,...]
    pallas_call x1, Pallas kernels: 19.5 us -> 16.8 us  [positions(): pl.pallas_call(positions_kernel, out_shape=(jax.ShapeDtypeStruct((2 * mod...]
    pallas_call x1, Pallas kernels: 20.6 us -> 18.5 us  [extended_of(): pl.pallas_call(halo_kernel, out_shape=jax.ShapeDtypeStruct((2, 3 * DET, 4...]
    unnamed x4 -> x10, local copies, waits for them, and re-layouts: 2.04 us -> 3.58 us
    pallas_call x1, Pallas kernels: 4.12 us -> 2.6 us  [orthonormal(): pl.pallas_call(ortho_kernel, out_shape=jax.ShapeDtypeStruct((24, 16, 8, D...]
where the time goes in v4:
time: 94.6 us; the launch traced here: 94.5 us
  Pallas kernels  90.2 us (95%)
  local copies, waits for them, and re-layouts  3.58 us (4%)
    pallas_call x1, Pallas kernels, reduced(): pl.pallas_call(reduce_kernel, out_shape=(jax.ShapeDtypeStruct((2, 12, 4,...  52.3 us
    pallas_call x1, Pallas kernels, extended_of(): pl.pallas_call(halo_kernel, out_shape=jax.ShapeDtypeStruct((2, 3 * DET, 4...  18.5 us
    pallas_call x1, Pallas kernels, positions(): pl.pallas_call(positions_kernel, out_shape=(jax.ShapeDtypeStruct((2 * mod...  16.8 us
    unnamed x10, local copies, waits for them, and re-layouts  3.58 us
    pallas_call x1, Pallas kernels, orthonormal(): pl.pallas_call(ortho_kernel, out_shape=jax.ShapeDtypeStruct((24, 16, 8, D...  2.6 us

profile of v4, /device:TPU:1, one launch (start us, length us, event | category | flops | bytes accessed | tf_op | source)
XLA Modules:
  0.0 94.5 jit_solution(7750812979835341193)
XLA Ops:
  0.6 0.0 copy-start
  0.6 0.9 copy.7.local_ref
  1.5 0.0 copy-start.1
  1.5 0.9 %copy-done.1 = f32[2,128,256]{2,1,0:T(8,128)S(1)} copy-done((f32[2,128,256]{2,1,0:T(8,128)S(1)}, f32[2,128,256]{2,1,0:T(8,128)}, u32[]{:S(2)}) %copy-start.1) | copy-done | bytes 262168
  2.5 0.0 copy-start.3
  2.5 18.5 %halo.1.ext_ref = f32[2,384,512]{2,1,0:T(8,128)S(1)} custom-call(f32[2,128,256]{2,1,0:T(8,128)S(1)} %copy-done.1), custom_call_target="tpu_custom_call" | custom-call | tf_op jit(solution)/shard_map/halo/pallas_call | solution.py:249
  21.0 0.0 copy-done
  21.0 0.0 copy-done.3
  21.0 0.0 copy-start.2
  21.0 1.0 %copy-done.2 = bf16[4,256,256]{2,1,0:T(8,128)(2,1)S(1)} copy-done((bf16[4,256,256]{2,1,0:T(8,128)(2,1)S(1)}, bf16[4,256,256]{2,1,0:T(8,128)(2,1)}, u32[]{:S(2)}) %copy-start.2) | copy-done | bytes 524312
  22.1 16.8 %positions.1 = (f32[26,128,128]{2,1,0:T(8,128)S(1)}, f32[3,384,512]{2,1,0:T(8,128)S(1)}) custom-call(s32[4,2]{1,0:T(4,128)S(1)} %copy.7.local_ref, f32[12,2,128,128]{3,2,1,0:T(8,128)S(1)} %copy-done, f32[4,128,128]{2,1,0:T(8,128)S(1)} %copy-done.3, f32[2,384,512]{2,1,0:T(8,128)S(1)} %halo.1.ext_ref, bf16[4,256,256]{2,1,0:T(8,128)(2,1)S(1)} %copy-done.2), custom_call_target="tpu_custom_call" | custom-call | tf_op jit(solution)/shard_map/positions/pallas_call | solution.py:150
  38.9 52.3 %reduce_all.1 = (f32[2,12,4,4,8,128]{5,4,3,2,1,0:T(8,128)S(1)}, f32[192,192]{1,0:T(8,128)S(1)}, f32[2,128,256]{2,1,0:T(8,128)S(1)}) custom-call(f32[2,13,4,4,8,128]{5,4,3,2,1,0:T(8,128)S(1)} %bitcast.5, f32[24,4,4,8,128]{4,3,2,1,0:T(8,128)S(1)} %bitcast.4, f32[3,384,512]{2,1,0:T(8,128)S(1)} %get-tuple-element.8.frame_ref, f32[2,128,256]{2,1,0:T(8,128)S(1)} %copy-done.1), custom_call_target="tpu_custom_call" | custom-call | tf_op jit(solution)/shard_map/reduce_all/pallas_call | solution.py:467
  91.2 2.6 %orthonormal.1 = f32[24,16,8,128]{3,2,1,0:T(8,128)} custom-call(f32[192,192]{1,0:T(8,128)S(1)} %get-tuple-element.9.mix_ref, f32[24,16,8,128]{3,2,1,0:T(8,128)S(1)} %bitcast.6), custom_call_target="tpu_custom_call" | custom-call | tf_op jit(solution)/shard_map/orthonormal/pallas_call | solution.py:542
  93.8 0.7 copy.9
Async XLA Ops:
  0.6 20.4 %copy-start = (f32[12,2,128,128]{3,2,1,0:T(8,128)S(1)}, f32[12,2,128,128]{3,2,1,0:T(8,128)}, u32[]{:S(2)}) copy-start(f32[12,2,128,128]{3,2,1,0:T(8,128)} %probe_ref.1) | copy-start | bytes 4718596
  1.5 0.9 %copy-start.1 = (f32[2,128,256]{2,1,0:T(8,128)S(1)}, f32[2,128,256]{2,1,0:T(8,128)}, u32[]{:S(2)}) copy-start(f32[2,128,256]{2,1,0:T(8,128)} %spec_ref.3) | copy-start | bytes 786436
  2.5 18.5 %copy-start.3 = (f32[4,128,128]{2,1,0:T(8,128)S(1)}, f32[4,128,128]{2,1,0:T(8,128)}, u32[]{:S(2)}) copy-start(f32[4,128,128]{2,1,0:T(8,128)} %patterns_ref.1) | copy-start | bytes 786436
  21.0 1.0 %copy-start.2 = (bf16[4,256,256]{2,1,0:T(8,128)(2,1)S(1)}, bf16[4,256,256]{2,1,0:T(8,128)(2,1)}, u32[]{:S(2)}) copy-start(bf16[4,256,256]{2,1,0:T(8,128)(2,1)} %constant.2.clone.tables_ref) | copy-start | bytes 1572868

commit v5 on v4

--- a/solution.py
+++ b/solution.py
@@ -44,29 +44,34 @@
     return jnp.dot(a, b, preferred_element_type=jnp.float32)
 
 
-def place(channel, modes):
-    return channel + channel // modes
-
-
 def window_of(local_ref, position):
-    row = local_ref[position, 0] - (lax.axis_index("scan") - 1) * DET
-    col = local_ref[position, 1] - (2 * lax.axis_index("tile") - 1) * DET
-    tile = jnp.minimum(col // DET, 2)
-    slab = jnp.minimum(row // 8, 31)
-    return pl.multiple_of(slab * 8, 8), row - slab * 8, pl.multiple_of(tile * DET, DET), col - tile * DET
-
-
-def positions_kernel(
+    row = local_ref[0, position] - (lax.axis_index("scan") - 1) * DET
+    col = local_ref[1, position] - (2 * lax.axis_index("tile") - 1) * DET
+    return row, col
+
+
+def swapped(value):
+    return jnp.concatenate(
+        [
+            jnp.concatenate([value[:DET, :DET], value[DET:, :DET]], axis=1),
+            jnp.concatenate([value[:DET, DET:], value[DET:, DET:]], axis=1),
+        ],
+        axis=0,
+    )
+
+
+def forward_kernel(
     local_ref,
     probe_ref,
     patterns_ref,
     ext_ref,
     tables_ref,
-    sums_ref,
-    frame_ref,
+    high_ref,
+    low_ref,
     patch_ref,
+    extra_ref,
+    light_ref,
     far_ref,
-    num_ref,
 ):
     modes = probe_ref.shape[0]
     pairs = modes // 2
@@ -74,32 +79,36 @@
     power = jnp.zeros((DET, DET), jnp.float32)
     for k in range(modes):
         power = power + probe_ref[k, 0] * probe_ref[k, 0] + probe_ref[k, 1] * probe_ref[k, 1]
-    sums_ref[...] = jnp.zeros_like(sums_ref)
-    frame_ref[...] = jnp.zeros_like(frame_ref)
+    extra_ref[...] = jnp.zeros_like(extra_ref)
+    light_ref[...] = jnp.zeros_like(light_ref)
+    for position in range(patterns_ref.shape[0]):
+        row, col = window_of(local_ref, position)
+        column = jnp.minimum(col // DET, 2)
+        slab = jnp.minimum(row // 8, 31)
+        shift, drop = col - column * DET, row - slab * 8
+        rows, cols = pl.ds(pl.multiple_of(slab * 8, 8), TALL), pl.ds(pl.multiple_of(column * DET, DET), 2 * DET)
+        for c in range(2):
+            window = pltpu.roll(ext_ref[c, rows, cols], lax.rem(2 * DET - shift, 2 * DET), 1)[:, :DET]
+            patch_ref[position, c] = pltpu.roll(window, lax.rem(TALL - drop, TALL), 0)[:DET]
+        value = jnp.concatenate([power, jnp.zeros((8, DET), jnp.float32)], axis=0)
+        value = pltpu.roll(value, drop, 0)
+        value = jnp.concatenate([value, jnp.zeros_like(value)], axis=1)
+        light_ref[rows, cols] += pltpu.roll(value, shift, 1)
+        ar, ai = patch_ref[position, 0], patch_ref[position, 1]
+        extra_ref[0] += ar * ar + ai * ai
+        extra_ref[1] += patterns_ref[position]
 
     def one_position(position, _):
-        slab, drop, tile, shift = window_of(local_ref, position)
-        for c in range(2):
-            window = ext_ref[c, pl.ds(slab, TALL), pl.ds(tile, 2 * DET)]
-            window = pltpu.roll(window, lax.rem(2 * DET - shift, 2 * DET), 1)[:, :DET]
-            patch_ref[c] = pltpu.roll(window, lax.rem(TALL - drop, TALL), 0)[:DET]
         model = jnp.zeros((DET, DET), jnp.float32)
         for j in range(pairs):
             lefts = []
             for k in (2 * j, 2 * j + 1):
                 pr, pi = probe_ref[k, 0], probe_ref[k, 1]
-                ar, ai = patch_ref[0], patch_ref[1]
+                ar, ai = patch_ref[position, 0], patch_ref[position, 1]
                 lefts.append(jnp.concatenate([pr * ar - pi * ai, pr * ai + pi * ar], axis=1))
             xh, xl = split(jnp.concatenate(lefts, axis=0))
             half = mm(xh, rh_ref[...]) + mm(xl, rh_ref[...]) + mm(xh, rl_ref[...])
-            half = jnp.concatenate(
-                [
-                    jnp.concatenate([half[:DET, :DET], half[DET:, :DET]], axis=1),
-                    jnp.concatenate([half[:DET, DET:], half[DET:, DET:]], axis=1),
-                ],
-                axis=0,
-            )
-            yh, yl = split(half)
+            yh, yl = split(swapped(half))
             far = mm(lh_ref[...], yh) + mm(lh_ref[...], yl) + mm(ll_ref[...], yh)
             far_ref[j] = far
             squares = far * far
@@ -108,68 +117,38 @@
         factor = jnp.sqrt(patterns_ref[position]) / jnp.sqrt(jnp.maximum(model, LIGHT_FLOOR)) - 1.0
         wide = jnp.concatenate([factor, factor], axis=1)
         wide = jnp.concatenate([wide, wide], axis=0)
-        num_ref[...] = jnp.zeros_like(num_ref)
         for j in range(pairs):
-            bh, bl = split(far_ref[j] * wide)
-            back = mm(rh_ref[...], bh) + mm(rh_ref[...], bl) + mm(rl_ref[...], bh)
-            back = jnp.concatenate(
-                [
-                    jnp.concatenate([back[:DET, :DET], back[DET:, :DET]], axis=1),
-                    jnp.concatenate([back[:DET, DET:], back[DET:, DET:]], axis=1),
-                ],
-                axis=0,
-            )
-            zh, zl = split(back)
-            change = mm(zh, lh_ref[...]) + mm(zl, lh_ref[...]) + mm(zh, ll_ref[...])
-            for i in range(2):
-                k = 2 * j + i
-                cr, ci = change[i * DET : i * DET + DET, :DET], change[i * DET : i * DET + DET, DET:]
-                pr, pi = probe_ref[k, 0], probe_ref[k, 1]
-                ar, ai = patch_ref[0], patch_ref[1]
-                at = place(2 * k, modes)
-                sums_ref[at] += ar * cr + ai * ci
-                sums_ref[at + 1] += ar * ci - ai * cr
-                num_ref[0] += pr * cr + pi * ci
-                num_ref[1] += pr * ci - pi * cr
-        ar, ai = patch_ref[0], patch_ref[1]
-        sums_ref[modes] += ar * ar + ai * ai
-        sums_ref[2 * modes + 1] += patterns_ref[position]
-        for c in range(3):
-            value = num_ref[c] if c < 2 else power
-            value = jnp.concatenate([value, jnp.zeros((8, DET), jnp.float32)], axis=0)
-            value = pltpu.roll(value, drop, 0)
-            value = jnp.concatenate([value, jnp.zeros_like(value)], axis=1)
-            frame_ref[c, pl.ds(slab, TALL), pl.ds(tile, 2 * DET)] += pltpu.roll(value, shift, 1)
+            high_ref[position, j], low_ref[position, j] = split(far_ref[j] * wide)
         return 0
 
     lax.fori_loop(0, patterns_ref.shape[0], one_position, 0)
 
 
-def positions(local, probe, patterns, extended):
-    modes = probe.shape[0]
+def forward(local, probe, patterns, extended, tables):
+    count, pairs = patterns.shape[0], probe.shape[0] // 2
+    spectra = jax.ShapeDtypeStruct((count, pairs, 2 * DET, 2 * DET), jnp.bfloat16)
     return pl.pallas_call(
-        positions_kernel,
+        forward_kernel,
         out_shape=(
-            jax.ShapeDtypeStruct((2 * modes + 2, DET, DET), jnp.float32),
-            jax.ShapeDtypeStruct((3,) + extended.shape[1:], jnp.float32),
+            spectra,
+            spectra,
+            jax.ShapeDtypeStruct((count, 2, DET, DET), jnp.float32),
+            jax.ShapeDtypeStruct((2, DET, DET), jnp.float32),
+            jax.ShapeDtypeStruct(extended.shape[1:], jnp.float32),
         ),
         in_specs=[SMEM] + [VMEM] * 4,
-        out_specs=(VMEM, VMEM),
-        scratch_shapes=[
-            pltpu.VMEM((2, DET, DET), jnp.float32),
-            pltpu.VMEM((modes // 2, 2 * DET, 2 * DET), jnp.float32),
-            pltpu.VMEM((2, DET, DET), jnp.float32),
-        ],
+        out_specs=(VMEM,) * 5,
+        scratch_shapes=[pltpu.VMEM((pairs, 2 * DET, 2 * DET), jnp.float32)],
         compiler_params=pltpu.CompilerParams(vmem_limit_bytes=LIMIT),
-        name="positions",
-    )(local, probe, patterns, extended, split_tables())
+        name="forward",
+    )(local, probe, patterns, extended, tables)
 
 
 def signal_all(peers):
     barrier = pltpu.get_barrier_semaphore()
     for peer in peers:
         pl.semaphore_signal(barrier, inc=1, device_id=peer, device_id_type=pl.DeviceIdType.MESH)
-    pl.semaphore_wait(barrier, len(peers))
+    return lambda: pl.semaphore_wait(barrier, len(peers))
 
 
 class Copies:
@@ -203,16 +182,17 @@
     return up, down, (scan, 1 - tile)
 
 
-def halo_kernel(spec_ref, ext_ref, send_sem, recv_sem):
+def halo_kernel(spec_ref, constants_ref, ext_ref, tables_ref, send_sem, recv_sem):
     scan, tile = lax.axis_index("scan"), lax.axis_index("tile")
     up, down, across = neighbours()
-    signal_all([up, down, across])
+    ready = signal_all([up, down, across])
     copies = Copies(send_sem, recv_sem)
     own, above, below = pl.ds(DET, DET), pl.ds(0, DET), pl.ds(2 * DET, DET)
     middle = pl.ds(DET, 2 * DET)
     given = pl.ds(pl.multiple_of((1 - tile) * DET, DET), DET)
     empty = pl.ds(pl.multiple_of(tile * 3 * DET, DET), DET)
     filled = pl.ds(pl.multiple_of((1 - tile) * 3 * DET, DET), DET)
+    ready()
     pieces = [(c, r * 64) for c in range(2) for r in range(2)]
     side = [
         copies.send(
@@ -225,6 +205,7 @@
         copies.send(spec_ref, ext_ref.at[:, above, middle], down),
     ]
     ext_ref[:, own, middle] = spec_ref[...]
+    tables_ref[...] = constants_ref[...]
     ext_ref[:, :, empty] = jnp.zeros((2, 3 * DET, DET), jnp.float32)
     for (c, r), copy in zip(pieces, side):
         copy.wait_recv()
@@ -248,13 +229,19 @@
 def extended_of(specimen):
     return pl.pallas_call(
         halo_kernel,
-        out_shape=jax.ShapeDtypeStruct((2, 3 * DET, 4 * DET), jnp.float32),
-        in_specs=[VMEM],
-        out_specs=VMEM,
-        scratch_shapes=[pltpu.SemaphoreType.DMA((14,)), pltpu.SemaphoreType.DMA((14,))],
+        out_shape=(
+            jax.ShapeDtypeStruct((2, 3 * DET, 4 * DET), jnp.float32),
+            jax.ShapeDtypeStruct((4, 2 * DET, 2 * DET), jnp.bfloat16),
+        ),
+        in_specs=[VMEM, VMEM],
+        out_specs=(VMEM, VMEM),
+        scratch_shapes=[
+            pltpu.SemaphoreType.DMA((14,)),
+            pltpu.SemaphoreType.DMA((14,)),
+        ],
         compiler_params=pltpu.CompilerParams(collective_id=1, has_side_effects=True, vmem_limit_bytes=LIMIT),
         name="halo",
-    )(specimen)
+    )(specimen, split_tables())
 
 
 SPLITS = ((0, 6), (6, 13))
@@ -292,16 +279,28 @@
     return {**here, axis: lax.rem(here[axis] + step, GRID[axis])}
 
 
+def slot_channel(slot):
+    mode = 2 * (slot // 2) if slot < 6 else 2 * ((slot - 6) // 2) + 1
+    return 2 * mode + slot % 2
+
+
 def reduce_kernel(
-    sums_ref,
+    local_ref,
+    high_ref,
+    low_ref,
+    patch_ref,
+    extra_ref,
+    light_ref,
+    tables_ref,
     probe_ref,
-    frame_ref,
-    spec_ref,
     upd_ref,
     mix_ref,
-    new_ref,
+    inside_ref,
+    given,
     held,
     work,
+    num_ref,
+    canvas,
     first_a,
     first_b,
     second_a,
@@ -324,7 +323,7 @@
     scan, tile = lax.axis_index("scan"), lax.axis_index("tile")
     up, down, across_tile = neighbours()
     peers = [moved(here, axis, step) for axis in ("x", "y", "z") for step in range(1, GRID[axis])]
-    signal_all([device_at(peer) for peer in peers + [partner]] + [up, down])
+    ready = signal_all([device_at(peer) for peer in peers + [partner]] + [up, down])
     copies = Copies(send_sem, recv_sem)
 
     def send(src, dst, peer):
@@ -333,54 +332,131 @@
     def around(axis):
         return [(step, moved(here, axis, step)) for step in range(1, GRID[axis])]
 
-    halves = []
-    for low, high in SPLITS:
-        rows = pl.ds(low, high - low)
-        halves.append(send(sums_ref.at[other, rows], held.at[rows], partner))
+    rh_ref, rl_ref, lh_ref, ll_ref = (tables_ref.at[i] for i in range(4))
+    count = patch_ref.shape[0]
+    num_ref[...] = jnp.zeros_like(num_ref)
+
+    def pair_step(side, pair, target):
+        slots = [2 * pair, 2 * pair + 1, 6 + 2 * pair, 7 + 2 * pair]
+        for slot in slots:
+            target[slot] = jnp.zeros((4, 4, 8, DET), jnp.float32)
+
+        def two_positions(step, _):
+            totals = [None] * 4
+            for q in range(2):
+                p = 2 * step + q
+                bh, bl = high_ref[p, 3 * side + pair], low_ref[p, 3 * side + pair]
+                back = mm(rh_ref[...], bh) + mm(rh_ref[...], bl) + mm(rl_ref[...], bh)
+                zh, zl = split(swapped(back))
+                change = mm(zh, lh_ref[...]) + mm(zl, lh_ref[...]) + mm(zh, ll_ref[...])
+                ar, ai = patch_ref[p, 0], patch_ref[p, 1]
+                for i in range(2):
+                    channel = 12 * side + 4 * pair + 2 * i
+                    cr = change[i * DET : i * DET + DET, :DET]
+                    ci = change[i * DET : i * DET + DET, DET:]
+                    pr = probe_ref[channel].reshape(DET, DET)
+                    pi = probe_ref[channel + 1].reshape(DET, DET)
+                    for c, value in enumerate((ar * cr + ai * ci, ar * ci - ai * cr)):
+                        old = totals[2 * i + c]
+                        totals[2 * i + c] = value if old is None else old + value
+                    num_ref[p, 0] += pr * cr + pi * ci
+                    num_ref[p, 1] += pr * ci - pi * cr
+            for slot, total in zip(slots, totals):
+                target[slot] += total.reshape(4, 4, 8, DET)
+            return 0
+
+        lax.fori_loop(0, count // 2, two_positions, 0)
+
+    def slots_of(pair):
+        return pl.ds(2 * pair, 2), pl.ds(6 + 2 * pair, 2)
+
     span = pl.ds(pl.multiple_of((1 - tile) * DET, DET), 3 * DET)
-    from_below = copies.send(frame_ref.at[:, pl.ds(0, DET), span], rows_in.at[0], up)
-    from_above = copies.send(frame_ref.at[:, pl.ds(2 * DET, DET), span], rows_in.at[1], down)
-    firsts = []
-    for half, (low, high) in enumerate(SPLITS):
-        halves[half].wait_recv()
-        rows = pl.ds(low, high - low)
-        work[rows] = sums_ref[core, rows] + held[rows]
-        if half == 0:
-            firsts.append(
-                [send(work.at[rows, p["x"]], first_a.at[i - 1], p) for i, p in around("x")]
-            )
-        else:
-            firsts.append(
-                [send(work.at[rows, :, p["y"]], first_b.at[i - 1], p) for i, p in around("y")]
-            )
-    seconds = []
+    top, bottom = pl.ds(0, DET), pl.ds(2 * DET, DET)
+    halves, firsts_a, firsts_b = [], [], []
+    last_slot = pl.ds(12, 1)
+
+    for pair in range(3):
+        pair_step(other, pair, given)
+        if pair == 0:
+            ready()
+            extra_half = send(extra_ref.at[pl.ds(other, 1)], held.at[last_slot], partner)
+            lights = [
+                copies.send(light_ref.at[top, span], rows_in.at[0, 2], up),
+                copies.send(light_ref.at[bottom, span], rows_in.at[1, 2], down),
+            ]
+        halves.append([send(given.at[s], held.at[s], partner) for s in slots_of(pair)])
+    extra_half.wait_recv()
+    work[12] = extra_ref[core] + held[12]
+    firsts_e = [send(work.at[last_slot, :, p["y"]], first_b.at[i - 1, pl.ds(6, 1)], p) for i, p in around("y")]
+
+    def fold_first(low, size, low_b, size_b):
+        rows, rows_b = pl.ds(low, size), pl.ds(6 + low_b, size_b)
+        from_b = pl.ds(low_b, size_b)
+        work[rows, x] += first_a[0, rows] + first_a[1, rows] + first_a[2, rows]
+        work[rows_b, :, y] += first_b[0, from_b] + first_b[1, from_b] + first_b[2, from_b]
+        a = [send(work.at[rows, x, p["y"]], second_a.at[i - 1, rows], p) for i, p in around("y")]
+        b = [send(work.at[rows_b, p["x"], y], second_b.at[i - 1, from_b], p) for i, p in around("x")]
+        return a + b
+
+    for pair in range(3):
+        pair_step(core, pair, work)
+        rows_a, rows_b = slots_of(pair)
+        for copy, rows in zip(halves[pair], (rows_a, rows_b)):
+            copy.wait_recv()
+            work[rows] += held[rows]
+        firsts_a.append(
+            [send(work.at[rows_a, p["x"]], first_a.at[i - 1, rows_a], p) for i, p in around("x")]
+        )
+        firsts_b.append(
+            [send(work.at[rows_b, :, p["y"]], first_b.at[i - 1, rows_a], p) for i, p in around("y")]
+        )
+    for copy in firsts_a[0] + firsts_a[1] + firsts_b[0] + firsts_b[1]:
+        copy.wait_recv()
+    seconds = fold_first(0, 4, 0, 4)
+
+    wide, tall = [], []
+    for p in range(count):
+        row, col = window_of(local_ref, p)
+        values = jnp.concatenate([num_ref[p, 0], num_ref[p, 1]], axis=0)
+        high, low = split(values)
+        place = lax.broadcasted_iota(jnp.int32, (DET, 4 * DET), 0) + col
+        across_shift = place == lax.broadcasted_iota(jnp.int32, (DET, 4 * DET), 1)
+        across_shift = jnp.where(across_shift, 1.0, 0.0).astype(jnp.bfloat16)
+        wide.append(split(mm(high, across_shift) + mm(low, across_shift)))
+        place = lax.broadcasted_iota(jnp.int32, (3 * DET, DET), 1) + row
+        down_shift = place == lax.broadcasted_iota(jnp.int32, (3 * DET, DET), 0)
+        tall.append(jnp.where(down_shift, 1.0, 0.0).astype(jnp.bfloat16))
+    down_shift = jnp.concatenate(tall, axis=1)
+    for c in range(2):
+        high = jnp.concatenate([w[0][c * DET : c * DET + DET] for w in wide], axis=0)
+        low = jnp.concatenate([w[1][c * DET : c * DET + DET] for w in wide], axis=0)
+        canvas[c] = mm(down_shift, high) + mm(down_shift, low)
+    rows_out = [
+        copies.send(canvas.at[:, top, span], rows_in.at[0, pl.ds(0, 2)], up),
+        copies.send(canvas.at[:, bottom, span], rows_in.at[1, pl.ds(0, 2)], down),
+    ]
+
+    for copy in firsts_a[2] + firsts_b[2] + firsts_e:
+        copy.wait_recv()
+    seconds += fold_first(4, 2, 4, 3)
+    for copy in seconds:
+        copy.wait_recv()
     rows_a, rows_b = (pl.ds(low, high - low) for low, high in SPLITS)
-    for copy in firsts[0]:
-        copy.wait_recv()
-    work[rows_a, x] += first_a[0] + first_a[1] + first_a[2]
-    seconds.append([send(work.at[rows_a, x, p["y"]], second_a.at[i - 1], p) for i, p in around("y")])
-    for copy in firsts[1]:
-        copy.wait_recv()
-    work[rows_b, :, y] += first_b[0] + first_b[1] + first_b[2]
-    seconds.append([send(work.at[rows_b, p["x"], y], second_b.at[i - 1], p) for i, p in around("x")])
-    for copy in seconds[0]:
-        copy.wait_recv()
     part[rows_a] = work[rows_a, x, y] + second_a[0] + second_a[1] + second_a[2]
-    for copy in seconds[1]:
-        copy.wait_recv()
     part[rows_b] = work[rows_b, x, y] + second_b[0] + second_b[1] + second_b[2]
     part[pl.ds(13, 3)] = jnp.zeros((3, 8, DET), jnp.float32)
 
     thirds = [
         send(part.at[pl.ds(2 * p["z"], 2)], third.at[i - 1], p) for i, p in around("z")
     ]
-    from_below.wait_recv()
-    from_above.wait_recv()
+    for copy in lights + rows_out:
+        copy.wait_recv()
     last_row = lax.axis_size("scan") - 1
     for c in range(3):
         added = jnp.where(scan == last_row, 0.0, rows_in[0, c])
         added = added + jnp.where(scan == 0, 0.0, rows_in[1, c])
-        frame[c] = frame_ref[c, pl.ds(DET, DET), span] + added
+        own = canvas[c, pl.ds(DET, DET), span] if c < 2 else light_ref[pl.ds(DET, DET), span]
+        frame[c] = own + added
     beyond = pl.ds(pl.multiple_of((1 - tile) * 2 * DET, DET), DET)
     sides = copies.send(frame.at[:, :, beyond], cols_in, across_tile)
     mine = part[pl.ds(2 * z, 2)]
@@ -397,11 +473,11 @@
 
     light = both[0, 12]
     power = jnp.zeros((8, DET), jnp.float32)
-    for channel in range(24):
-        old = probe_ref[channel, x, y]
-        power = power + old * old
-        new = old + both[channel // 12, channel % 12] / (light + PROBE_REG)
-        block[channel // 12, pl.ds(8 * (channel % 12), 8)] = new
+    for c in range(2):
+        for slot in range(12):
+            old = probe_ref[12 * c + slot_channel(slot), x, y]
+            power = power + old * old
+            block[c, pl.ds(8 * slot, 8)] = old + both[c, slot] / (light + PROBE_REG)
     for i in range(12):
         upd_ref[core, i, x, y] = block[core, pl.ds(8 * i, 8)]
     rows = jnp.concatenate(
@@ -440,13 +516,11 @@
         copy.wait_recv()
     mix_ref[...] = expanded(mixing((grams[1, 0] + grams[1, 1]) + (grams[1, 2] + grams[1, 3])))
     sides.wait_recv()
-    inside = [frame[c, :, pl.ds(pl.multiple_of(tile * DET, DET), 2 * DET)] for c in range(3)]
     for c in range(3):
         left = jnp.where(tile == 1, cols_in[c], 0.0)
         right = jnp.where(tile == 0, cols_in[c], 0.0)
-        inside[c] = inside[c] + jnp.concatenate([left, right], axis=1)
-    for c in range(2):
-        new_ref[c] = spec_ref[c] + inside[c] / (inside[2] + OBJECT_REG)
+        own = frame[c, :, pl.ds(pl.multiple_of(tile * DET, DET), 2 * DET)]
+        inside_ref[c] = own + jnp.concatenate([left, right], axis=1)
     for step in range(1, 4):
         far_a[step - 1].wait_recv()
         got = upd_ref.at[core, one_a, lax.rem(x + 4 - step, 4)]
@@ -459,23 +533,27 @@
     copies.finish()
 
 
-COPIES = 58
-
-
-def reduced(sums, probe, frame, specimen):
+COPIES = 96
+
+
+def reduced(local, spectra, tables, probe):
     f32 = jnp.float32
+    high, low, patches, extra, light = spectra
     return pl.pallas_call(
         reduce_kernel,
         out_shape=(
             jax.ShapeDtypeStruct((2, 12, 4, 4, 8, DET), f32),
             jax.ShapeDtypeStruct((192, 192), f32),
-            jax.ShapeDtypeStruct(specimen.shape, f32),
+            jax.ShapeDtypeStruct((3, DET, 2 * DET), f32),
         ),
-        in_specs=[VMEM] * 4,
+        in_specs=[SMEM] + [VMEM] * 7,
         out_specs=(VMEM,) * 3,
         scratch_shapes=[
+            pltpu.VMEM((12, 4, 4, 8, DET), f32),
             pltpu.VMEM((13, 4, 4, 8, DET), f32),
             pltpu.VMEM((13, 4, 4, 8, DET), f32),
+            pltpu.VMEM((4, 2, DET, DET), f32),
+            pltpu.VMEM((2, 3 * DET, 4 * DET), f32),
             pltpu.VMEM((3, 6, 4, 8, DET), f32),
             pltpu.VMEM((3, 7, 4, 8, DET), f32),
             pltpu.VMEM((3, 6, 8, DET), f32),
@@ -491,9 +569,20 @@
             pltpu.SemaphoreType.DMA((COPIES,)),
             pltpu.SemaphoreType.DMA((COPIES,)),
         ],
-        compiler_params=pltpu.CompilerParams(collective_id=0, has_side_effects=True, vmem_limit_bytes=LIMIT),
+        compiler_params=pltpu.CompilerParams(
+            collective_id=0, has_side_effects=True, vmem_limit_bytes=LIMIT
+        ),
         name="reduce_all",
-    )(sums.reshape(2, 13, 4, 4, 8, DET), probe.reshape(24, 4, 4, 8, DET), frame, specimen)
+    )(
+        local,
+        high,
+        low,
+        patches,
+        extra.reshape(2, 4, 4, 8, DET),
+        light,
+        tables,
+        probe.reshape(24, 4, 4, 8, DET),
+    )
 
 
 def mixing(gram):
@@ -529,32 +618,41 @@
     return jnp.where(lax.rem(row, 8) == lax.rem(col, 8), large, 0.0)
 
 
-def ortho_kernel(mix_ref, upd_ref, out_ref):
+def finish_kernel(mix_ref, upd_ref, inside_ref, spec_ref, out_ref, new_ref):
     large = mix_ref[...]
     for b in range(0, 16, 2):
         blocks = [upd_ref[:, b + i].reshape(192, DET) for i in range(2)]
         result = dot32(large, jnp.concatenate(blocks, axis=1))
         for i in range(2):
-            out_ref[:, b + i] = result[:, i * DET : i * DET + DET].reshape(24, 8, DET)
-
-
-def orthonormal(mix, updated):
+            block = result[:, i * DET : i * DET + DET].reshape(24, 8, DET)
+            for c in range(2):
+                for slot in range(12):
+                    out_ref[12 * c + slot_channel(slot), b + i] = block[12 * c + slot]
+    for c in range(2):
+        new_ref[c] = spec_ref[c] + inside_ref[c] / (inside_ref[2] + OBJECT_REG)
+
+
+def finished(mix, updated, inside, specimen):
     return pl.pallas_call(
-        ortho_kernel,
-        out_shape=jax.ShapeDtypeStruct((24, 16, 8, DET), jnp.float32),
-        in_specs=[VMEM, VMEM],
-        out_specs=VMEM,
+        finish_kernel,
+        out_shape=(
+            jax.ShapeDtypeStruct((24, 16, 8, DET), jnp.float32),
+            jax.ShapeDtypeStruct(specimen.shape, jnp.float32),
+        ),
+        in_specs=[VMEM] * 4,
+        out_specs=(VMEM, VMEM),
         compiler_params=pltpu.CompilerParams(vmem_limit_bytes=LIMIT),
-        name="orthonormal",
-    )(mix, updated.reshape(24, 16, 8, DET))
+        name="finish",
+    )(mix, updated.reshape(24, 16, 8, DET), inside, specimen)
 
 
 def body(probe_modes, patterns, specimen, offsets):
-    extended = extended_of(specimen)
-    sums, frame = positions(offsets, probe_modes, patterns, extended)
-    updated, mix, new_specimen = reduced(sums, probe_modes, frame, specimen)
-    new_probe = orthonormal(mix, updated).reshape(probe_modes.shape)
-    return (new_probe, new_specimen)
+    local = offsets.T
+    extended, tables = extended_of(specimen)
+    spectra = forward(local, probe_modes, patterns, extended, tables)
+    updated, mix, inside = reduced(local, spectra, tables, probe_modes)
+    new_probe, new_specimen = finished(mix, updated, inside, specimen)
+    return (new_probe.reshape(probe_modes.shape), new_specimen)
 
 
 def solution(mesh):

time: 94.6 us -> 90.5 us (0.957)
  Pallas kernels: 90.2 us -> 84.5 us
  local copies, waits for them, and re-layouts: 3.58 us -> 5.02 us
    pallas_call x3, Pallas kernels: 37.9 us -> 30.6 us  [the longest x1 18.5 us: extended_of(): pl.pallas_call(halo_kernel, out_shape=(jax.ShapeDtypeStruct((2, 3 * DET,...]
    pallas_call x1, Pallas kernels: 52.3 us -> 54 us  [reduced(): pl.pallas_call(reduce_kernel, out_shape=(jax.ShapeDtypeStruct((2, 12, 4,...]
    unnamed x10 -> x12, local copies, waits for them, and re-layouts: 3.58 us -> 5.02 us
where the time goes in v5:
time: 90.5 us; the launch traced here: 90.2 us
  Pallas kernels  84.5 us (93%)
  local copies, waits for them, and re-layouts  5.02 us (6%)
    pallas_call x1, Pallas kernels, reduced(): pl.pallas_call(reduce_kernel, out_shape=(jax.ShapeDtypeStruct((2, 12, 4,...  54 us
    pallas_call x1, Pallas kernels, extended_of(): pl.pallas_call(halo_kernel, out_shape=(jax.ShapeDtypeStruct((2, 3 * DET,...  18.5 us
    pallas_call x1, Pallas kernels, forward(): pl.pallas_call(forward_kernel, out_shape=(spectra, spectra, jax.ShapeDtyp...  9.42 us
    unnamed x12, local copies, waits for them, and re-layouts  5.02 us
    pallas_call x1, Pallas kernels, finished(): pl.pallas_call(finish_kernel, out_shape=(jax.ShapeDtypeStruct((24, 16, 8,...  2.65 us

profile of v5, /device:TPU:1, one launch (start us, length us, event | category | flops | bytes accessed | tf_op | source)
XLA Modules:
  0.0 90.2 jit_solution(10945423066050213297)
XLA Ops:
  0.6 0.0 copy-start.2
  0.6 0.9 %copy-done.2 = f32[2,128,256]{2,1,0:T(8,128)S(1)} copy-done((f32[2,128,256]{2,1,0:T(8,128)S(1)}, f32[2,128,256]{2,1,0:T(8,128)}, u32[]{:S(2)}) %copy-start.2) | copy-done | bytes 262168
  1.6 0.0 copy-start.3
  1.6 1.0 %copy-done.3 = bf16[4,256,256]{2,1,0:T(8,128)(2,1)S(1)} copy-done((bf16[4,256,256]{2,1,0:T(8,128)(2,1)S(1)}, bf16[4,256,256]{2,1,0:T(8,128)(2,1)}, u32[]{:S(2)}) %copy-start.3) | copy-done | bytes 524312
  2.6 18.5 %halo.1 = (f32[2,384,512]{2,1,0:T(8,128)S(1)}, bf16[4,256,256]{2,1,0:T(8,128)(2,1)S(1)}) custom-call(f32[2,128,256]{2,1,0:T(8,128)S(1)} %copy-done.2, bf16[4,256,256]{2,1,0:T(8,128)(2,1)S(1)} %copy-done.3), custom_call_target="tpu_custom_call" | custom-call | tf_op jit(solution)/shard_map/halo/pallas_call | solution.py:230
  21.1 0.0 copy-start
  21.1 1.4 %copy-done = f32[12,2,128,128]{3,2,1,0:T(8,128)S(1)} copy-done((f32[12,2,128,128]{3,2,1,0:T(8,128)S(1)}, f32[12,2,128,128]{3,2,1,0:T(8,128)}, u32[]{:S(2)}) %copy-start) | copy-done | bytes 1572888
  22.5 0.0 copy-start.4
  22.5 0.9 %copy-done.4 = f32[4,128,128]{2,1,0:T(8,128)S(1)} copy-done((f32[4,128,128]{2,1,0:T(8,128)S(1)}, f32[4,128,128]{2,1,0:T(8,128)}, u32[]{:S(2)}) %copy-start.4) | copy-done | bytes 262168
  23.5 0.0 copy-start.5
  23.5 0.7 copy-done.5
  24.2 0.0 copy-start.1
  24.2 9.4 %forward.1 = (bf16[4,6,256,256]{3,2,1,0:T(8,128)(2,1)S(1)}, bf16[4,6,256,256]{3,2,1,0:T(8,128)(2,1)S(1)}, f32[4,2,128,128]{3,2,1,0:T(8,128)S(1)}, f32[2,128,128]{2,1,0:T(8,128)S(1)}, f32[384,512]{1,0:T(8,128)S(1)}) custom-call(s32[2,4]{1,0:T(2,128)S(1)} %bitcast.8, f32[12,2,128,128]{3,2,1,0:T(8,128)S(1)} %copy-done, f32[4,128,128]{2,1,0:T(8,128)S(1)} %copy-done.4, ...), custom_call_target="tpu_custom_call" | custom-call | tf_op jit(solution)/shard_map/forward/pallas_call | solution.py:130
  33.6 0.0 copy-done.1
  33.6 54.0 %reduce_all.1 = (f32[2,12,4,4,8,128]{5,4,3,2,1,0:T(8,128)S(1)}, f32[192,192]{1,0:T(8,128)S(1)}, f32[3,128,256]{2,1,0:T(8,128)S(1)}) custom-call(s32[2,4]{1,0:T(2,128)S(1)} %bitcast.9, bf16[4,6,256,256]{3,2,1,0:T(8,128)(2,1)S(1)} %get-tuple-element.16.high_ref, bf16[4,6,256,256]{3,2,1,0:T(8,128)(2,1)S(1)} %get-tuple-element.17.low_ref, ...), custom_call_target="tpu_custom_call" | custom-call | tf_op jit(solution)/shard_map/reduce_all/pallas_call | solution.py:542
  87.6 2.6 %finish.1 = (f32[24,16,8,128]{3,2,1,0:T(8,128)}, f32[2,128,256]{2,1,0:T(8,128)}) custom-call(f32[192,192]{1,0:T(8,128)S(1)} %get-tuple-element.21.mix_ref, f32[24,16,8,128]{3,2,1,0:T(8,128)S(1)} %bitcast.6, f32[3,128,256]{2,1,0:T(8,128)S(1)} %get-tuple-element.23.inside_ref, f32[2,128,256]{2,1,0:T(8,128)S(1)} %copy-done.2), custom_call_target="tpu_custom_call" | custom-call | tf_op jit(solution)/shard_map/finish/pallas_call | solution.py:636
Async XLA Ops:
  0.6 1.0 %copy-start.2 = (f32[2,128,256]{2,1,0:T(8,128)S(1)}, f32[2,128,256]{2,1,0:T(8,128)}, u32[]{:S(2)}) copy-start(f32[2,128,256]{2,1,0:T(8,128)} %spec_ref.3) | copy-start | bytes 786436
  1.6 1.0 %copy-start.3 = (bf16[4,256,256]{2,1,0:T(8,128)(2,1)S(1)}, bf16[4,256,256]{2,1,0:T(8,128)(2,1)}, u32[]{:S(2)}) copy-start(bf16[4,256,256]{2,1,0:T(8,128)(2,1)} %constant.2.clone.constants_ref) | copy-start | bytes 1572868
  21.1 1.4 %copy-start = (f32[12,2,128,128]{3,2,1,0:T(8,128)S(1)}, f32[12,2,128,128]{3,2,1,0:T(8,128)}, u32[]{:S(2)}) copy-start(f32[12,2,128,128]{3,2,1,0:T(8,128)} %probe_ref.1) | copy-start | bytes 4718596
  22.5 0.9 %copy-start.4 = (f32[4,128,128]{2,1,0:T(8,128)S(1)}, f32[4,128,128]{2,1,0:T(8,128)}, u32[]{:S(2)}) copy-start(f32[4,128,128]{2,1,0:T(8,128)} %patterns_ref.1) | copy-start | bytes 786436
  23.5 0.7 copy-start.5
  24.2 9.4 %copy-start.1 = (f32[12,2,128,128]{3,2,1,0:T(8,128)S(1)}, f32[12,2,128,128]{3,2,1,0:T(8,128)}, u32[]{:S(2)}) copy-start(f32[12,2,128,128]{3,2,1,0:T(8,128)} %probe_ref.1) | copy-start | bytes 4718596

commit v6 on v5

--- a/solution.py
+++ b/solution.py
@@ -13,6 +13,8 @@
 DET = 128
 TALL = 136
 LIMIT = 20 * 2**20
+FLOPS_PER_US = 10**9
+BYTES_PER_US = 3 * 10**6
 LIGHT_FLOOR = 0.05
 OBJECT_REG = 0.5
 PROBE_REG = 1.0
@@ -20,6 +22,14 @@
 VMEM = pl.BlockSpec(memory_space=pltpu.VMEM)
 SMEM = pl.BlockSpec(memory_space=pltpu.SMEM)
 highest = lax.Precision.HIGHEST
+
+
+def cost(microseconds):
+    return pl.CostEstimate(
+        flops=int(microseconds * FLOPS_PER_US),
+        bytes_accessed=int(microseconds * BYTES_PER_US),
+        transcendentals=0,
+    )
 
 
 def split_tables():
@@ -138,6 +148,7 @@
         ),
         in_specs=[SMEM] + [VMEM] * 4,
         out_specs=(VMEM,) * 5,
+        cost_estimate=cost(9),
         scratch_shapes=[pltpu.VMEM((pairs, 2 * DET, 2 * DET), jnp.float32)],
         compiler_params=pltpu.CompilerParams(vmem_limit_bytes=LIMIT),
         name="forward",
@@ -182,7 +193,7 @@
     return up, down, (scan, 1 - tile)
 
 
-def halo_kernel(spec_ref, constants_ref, ext_ref, tables_ref, send_sem, recv_sem):
+def halo_kernel(spec_ref, ext_ref, send_sem, recv_sem):
     scan, tile = lax.axis_index("scan"), lax.axis_index("tile")
     up, down, across = neighbours()
     ready = signal_all([up, down, across])
@@ -205,7 +216,6 @@
         copies.send(spec_ref, ext_ref.at[:, above, middle], down),
     ]
     ext_ref[:, own, middle] = spec_ref[...]
-    tables_ref[...] = constants_ref[...]
     ext_ref[:, :, empty] = jnp.zeros((2, 3 * DET, DET), jnp.float32)
     for (c, r), copy in zip(pieces, side):
         copy.wait_recv()
@@ -229,19 +239,17 @@
 def extended_of(specimen):
     return pl.pallas_call(
         halo_kernel,
-        out_shape=(
-            jax.ShapeDtypeStruct((2, 3 * DET, 4 * DET), jnp.float32),
-            jax.ShapeDtypeStruct((4, 2 * DET, 2 * DET), jnp.bfloat16),
-        ),
-        in_specs=[VMEM, VMEM],
-        out_specs=(VMEM, VMEM),
+        out_shape=jax.ShapeDtypeStruct((2, 3 * DET, 4 * DET), jnp.float32),
+        in_specs=[VMEM],
+        out_specs=VMEM,
+        cost_estimate=cost(8),
         scratch_shapes=[
             pltpu.SemaphoreType.DMA((14,)),
             pltpu.SemaphoreType.DMA((14,)),
         ],
         compiler_params=pltpu.CompilerParams(collective_id=1, has_side_effects=True, vmem_limit_bytes=LIMIT),
         name="halo",
-    )(specimen, split_tables())
+    )(specimen)
 
 
 SPLITS = ((0, 6), (6, 13))
@@ -547,6 +555,7 @@
             jax.ShapeDtypeStruct((3, DET, 2 * DET), f32),
         ),
         in_specs=[SMEM] + [VMEM] * 7,
+        cost_estimate=cost(45),
         out_specs=(VMEM,) * 3,
         scratch_shapes=[
             pltpu.VMEM((12, 4, 4, 8, DET), f32),
@@ -641,6 +650,7 @@
         ),
         in_specs=[VMEM] * 4,
         out_specs=(VMEM, VMEM),
+        cost_estimate=cost(3),
         compiler_params=pltpu.CompilerParams(vmem_limit_bytes=LIMIT),
         name="finish",
     )(mix, updated.reshape(24, 16, 8, DET), inside, specimen)
@@ -648,7 +658,7 @@
 
 def body(probe_modes, patterns, specimen, offsets):
     local = offsets.T
-    extended, tables = extended_of(specimen)
+    extended, tables = extended_of(specimen), split_tables()
     spectra = forward(local, probe_modes, patterns, extended, tables)
     updated, mix, inside = reduced(local, spectra, tables, probe_modes)
     new_probe, new_specimen = finished(mix, updated, inside, specimen)

time: 90.5 us -> 86.8 us (0.959)
  local copies, waits for them, and re-layouts: 5.02 us -> 0.97 us
    unnamed x12, local copies, waits for them, and re-layouts: 5.02 us -> 0.97 us
where the time goes in v6:
time: 86.8 us; the launch traced here: 86.7 us
  Pallas kernels  85.1 us (98%)
  local copies, waits for them, and re-layouts  0.97 us (1%)
    pallas_call x1, Pallas kernels, reduced(): pl.pallas_call(reduce_kernel, out_shape=(jax.ShapeDtypeStruct((2, 12, 4,...  54.1 us
    pallas_call x1, Pallas kernels, extended_of(): pl.pallas_call(halo_kernel, out_shape=jax.ShapeDtypeStruct((2, 3 * DET, 4...  18.7 us
    pallas_call x1, Pallas kernels, forward(): pl.pallas_call(forward_kernel, out_shape=(spectra, spectra, jax.ShapeDtyp...  9.66 us
    pallas_call x1, Pallas kernels, finished(): pl.pallas_call(finish_kernel, out_shape=(jax.ShapeDtypeStruct((24, 16, 8,...  2.65 us

profile of v6, /device:TPU:1, one launch (start us, length us, event | category | flops | bytes accessed | tf_op | source)
XLA Modules:
  0.0 86.7 jit_solution(5395241527323660537)
XLA Ops:
  0.6 0.0 copy-start.2
  0.6 0.9 %copy-done.2 = f32[2,128,256]{2,1,0:T(8,128)S(1)} copy-done((f32[2,128,256]{2,1,0:T(8,128)S(1)}, f32[2,128,256]{2,1,0:T(8,128)}, u32[]{:S(2)}) %copy-start.2) | copy-done | bytes 262168
  1.6 0.0 copy-start
  1.6 0.0 copy-start.1
  1.6 0.0 copy-start.4
  1.6 0.0 copy-start.5
  1.6 18.7 %halo.1.ext_ref = f32[2,384,512]{2,1,0:T(8,128)S(1)} custom-call(f32[2,128,256]{2,1,0:T(8,128)S(1)} %copy-done.2), custom_call_target="tpu_custom_call" | custom-call | flops 8000000000 | bytes 24000000 | tf_op jit(solution)/shard_map/halo/pallas_call | solution.py:240
  20.3 0.0 copy-done
  20.3 0.0 copy-done.1
  20.3 0.0 copy-done.4
  20.3 0.0 copy-done.5
  20.3 9.7 %forward.1 = (bf16[4,6,256,256]{3,2,1,0:T(8,128)(2,1)S(1)}, bf16[4,6,256,256]{3,2,1,0:T(8,128)(2,1)S(1)}, f32[4,2,128,128]{3,2,1,0:T(8,128)S(1)}, f32[2,128,128]{2,1,0:T(8,128)S(1)}, f32[384,512]{1,0:T(8,128)S(1)}) custom-call(s32[2,4]{1,0:T(2,128)S(1)} %bitcast.6, f32[12,2,128,128]{3,2,1,0:T(8,128)S(1)} %copy-done, f32[4,128,128]{2,1,0:T(8,128)S(1)} %copy-done.1, ...), custom_call_target="tpu_custom_call" | custom-call | flops 8999999488 | bytes 27000000 | tf_op jit(solution)/shard_map/forward/pallas_call | solution.py:140
  30.0 0.0 copy-start.3
  30.0 54.1 %reduce_all.1 = (f32[2,12,4,4,8,128]{5,4,3,2,1,0:T(8,128)S(1)}, f32[192,192]{1,0:T(8,128)S(1)}, f32[3,128,256]{2,1,0:T(8,128)S(1)}) custom-call(s32[2,4]{1,0:T(2,128)S(1)} %bitcast.7, bf16[4,6,256,256]{3,2,1,0:T(8,128)(2,1)S(1)} %get-tuple-element.12.high_ref, bf16[4,6,256,256]{3,2,1,0:T(8,128)(2,1)S(1)} %get-tuple-element.13.low_ref, ...), custom_call_target="tpu_custom_call" | custom-call | flops 44999999488 | bytes 135000000 | tf_op jit(solution)/shard_map/reduce_all/pallas_call | solution.py:550
  84.1 0.0 copy-done.3
  84.1 2.6 %finish.1 = (f32[24,16,8,128]{3,2,1,0:T(8,128)}, f32[2,128,256]{2,1,0:T(8,128)}) custom-call(f32[192,192]{1,0:T(8,128)S(1)} %get-tuple-element.17.mix_ref, f32[24,16,8,128]{3,2,1,0:T(8,128)S(1)} %bitcast.8, f32[3,128,256]{2,1,0:T(8,128)S(1)} %get-tuple-element.19.inside_ref, f32[2,128,256]{2,1,0:T(8,128)S(1)} %copy-done.3), custom_call_target="tpu_custom_call" | custom-call | flops 3000000000 | bytes 9000000 | tf_op jit(solution)/shard_map/finish/pallas_call | solution.py:645
Async XLA Ops:
  0.6 1.0 %copy-start.2 = (f32[2,128,256]{2,1,0:T(8,128)S(1)}, f32[2,128,256]{2,1,0:T(8,128)}, u32[]{:S(2)}) copy-start(f32[2,128,256]{2,1,0:T(8,128)} %spec_ref.3) | copy-start | bytes 786436
  1.6 18.7 %copy-start = (f32[12,2,128,128]{3,2,1,0:T(8,128)S(1)}, f32[12,2,128,128]{3,2,1,0:T(8,128)}, u32[]{:S(2)}) copy-start(f32[12,2,128,128]{3,2,1,0:T(8,128)} %probe_ref.1) | copy-start | bytes 4718596
  1.6 18.7 %copy-start.1 = (f32[4,128,128]{2,1,0:T(8,128)S(1)}, f32[4,128,128]{2,1,0:T(8,128)}, u32[]{:S(2)}) copy-start(f32[4,128,128]{2,1,0:T(8,128)} %patterns_ref.1) | copy-start | bytes 786436
  1.6 18.7 %copy-start.4 = (s32[4,2]{0,1:T(2,128)S(1)}, s32[4,2]{0,1:T(2,128)}, u32[]{:S(2)}) copy-start(s32[4,2]{0,1:T(2,128)} %param.8) | copy-start | bytes 100
  1.6 18.7 %copy-start.5 = (bf16[4,256,256]{2,1,0:T(8,128)(2,1)S(1)}, bf16[4,256,256]{2,1,0:T(8,128)(2,1)}, u32[]{:S(2)}) copy-start(bf16[4,256,256]{2,1,0:T(8,128)(2,1)} %constant.2.clone.tables_ref) | copy-start | bytes 1572868
  30.0 54.1 %copy-start.3 = (f32[2,128,256]{2,1,0:T(8,128)S(1)}, f32[2,128,256]{2,1,0:T(8,128)}, u32[]{:S(2)}) copy-start(f32[2,128,256]{2,1,0:T(8,128)} %spec_ref.3) | copy-start | bytes 786436

commit v7 on v6

--- a/solution.py
+++ b/solution.py
@@ -82,6 +82,8 @@
     extra_ref,
     light_ref,
     far_ref,
+    half_high,
+    half_low,
 ):
     modes = probe_ref.shape[0]
     pairs = modes // 2
@@ -109,16 +111,18 @@
         extra_ref[1] += patterns_ref[position]
 
     def one_position(position, _):
-        model = jnp.zeros((DET, DET), jnp.float32)
+        ar, ai = patch_ref[position, 0], patch_ref[position, 1]
         for j in range(pairs):
             lefts = []
             for k in (2 * j, 2 * j + 1):
                 pr, pi = probe_ref[k, 0], probe_ref[k, 1]
-                ar, ai = patch_ref[position, 0], patch_ref[position, 1]
                 lefts.append(jnp.concatenate([pr * ar - pi * ai, pr * ai + pi * ar], axis=1))
             xh, xl = split(jnp.concatenate(lefts, axis=0))
             half = mm(xh, rh_ref[...]) + mm(xl, rh_ref[...]) + mm(xh, rl_ref[...])
-            yh, yl = split(swapped(half))
+            half_high[j], half_low[j] = split(swapped(half))
+        model = jnp.zeros((DET, DET), jnp.float32)
+        for j in range(pairs):
+            yh, yl = half_high[j], half_low[j]
             far = mm(lh_ref[...], yh) + mm(lh_ref[...], yl) + mm(ll_ref[...], yh)
             far_ref[j] = far
             squares = far * far
@@ -149,7 +153,11 @@
         in_specs=[SMEM] + [VMEM] * 4,
         out_specs=(VMEM,) * 5,
         cost_estimate=cost(9),
-        scratch_shapes=[pltpu.VMEM((pairs, 2 * DET, 2 * DET), jnp.float32)],
+        scratch_shapes=[
+            pltpu.VMEM((pairs, 2 * DET, 2 * DET), jnp.float32),
+            pltpu.VMEM((pairs, 2 * DET, 2 * DET), jnp.bfloat16),
+            pltpu.VMEM((pairs, 2 * DET, 2 * DET), jnp.bfloat16),
+        ],
         compiler_params=pltpu.CompilerParams(vmem_limit_bytes=LIMIT),
         name="forward",
     )(local, probe, patterns, extended, tables)
@@ -308,6 +316,8 @@
     held,
     work,
     num_ref,
+    back_high,
+    back_low,
     canvas,
     first_a,
     first_b,
@@ -346,34 +356,28 @@
 
     def pair_step(side, pair, target):
         slots = [2 * pair, 2 * pair + 1, 6 + 2 * pair, 7 + 2 * pair]
-        for slot in slots:
-            target[slot] = jnp.zeros((4, 4, 8, DET), jnp.float32)
-
-        def two_positions(step, _):
-            totals = [None] * 4
-            for q in range(2):
-                p = 2 * step + q
-                bh, bl = high_ref[p, 3 * side + pair], low_ref[p, 3 * side + pair]
-                back = mm(rh_ref[...], bh) + mm(rh_ref[...], bl) + mm(rl_ref[...], bh)
-                zh, zl = split(swapped(back))
-                change = mm(zh, lh_ref[...]) + mm(zl, lh_ref[...]) + mm(zh, ll_ref[...])
-                ar, ai = patch_ref[p, 0], patch_ref[p, 1]
-                for i in range(2):
-                    channel = 12 * side + 4 * pair + 2 * i
-                    cr = change[i * DET : i * DET + DET, :DET]
-                    ci = change[i * DET : i * DET + DET, DET:]
-                    pr = probe_ref[channel].reshape(DET, DET)
-                    pi = probe_ref[channel + 1].reshape(DET, DET)
-                    for c, value in enumerate((ar * cr + ai * ci, ar * ci - ai * cr)):
-                        old = totals[2 * i + c]
-                        totals[2 * i + c] = value if old is None else old + value
-                    num_ref[p, 0] += pr * cr + pi * ci
-                    num_ref[p, 1] += pr * ci - pi * cr
-            for slot, total in zip(slots, totals):
-                target[slot] += total.reshape(4, 4, 8, DET)
-            return 0
-
-        lax.fori_loop(0, count // 2, two_positions, 0)
+        for p in range(count):
+            bh, bl = high_ref[p, 3 * side + pair], low_ref[p, 3 * side + pair]
+            back = mm(rh_ref[...], bh) + mm(rh_ref[...], bl) + mm(rl_ref[...], bh)
+            back_high[p], back_low[p] = split(swapped(back))
+        for p in range(count):
+            zh, zl = back_high[p], back_low[p]
+            change = mm(zh, lh_ref[...]) + mm(zl, lh_ref[...]) + mm(zh, ll_ref[...])
+            ar, ai = patch_ref[p, 0], patch_ref[p, 1]
+            nums = [num_ref[p, 0], num_ref[p, 1]]
+            for i in range(2):
+                channel = 12 * side + 4 * pair + 2 * i
+                cr = change[i * DET : i * DET + DET, :DET]
+                ci = change[i * DET : i * DET + DET, DET:]
+                pr = probe_ref[channel].reshape(DET, DET)
+                pi = probe_ref[channel + 1].reshape(DET, DET)
+                for c, value in enumerate((ar * cr + ai * ci, ar * ci - ai * cr)):
+                    value = value.reshape(4, 4, 8, DET)
+                    slot = slots[2 * i + c]
+                    target[slot] = value if p == 0 else target[slot] + value
+                nums[0] += pr * cr + pi * ci
+                nums[1] += pr * ci - pi * cr
+            num_ref[p, 0], num_ref[p, 1] = nums
 
     def slots_of(pair):
         return pl.ds(2 * pair, 2), pl.ds(6 + 2 * pair, 2)
@@ -562,6 +566,8 @@
             pltpu.VMEM((13, 4, 4, 8, DET), f32),
             pltpu.VMEM((13, 4, 4, 8, DET), f32),
             pltpu.VMEM((4, 2, DET, DET), f32),
+            pltpu.VMEM((4, 2 * DET, 2 * DET), jnp.bfloat16),
+            pltpu.VMEM((4, 2 * DET, 2 * DET), jnp.bfloat16),
             pltpu.VMEM((2, 3 * DET, 4 * DET), f32),
             pltpu.VMEM((3, 6, 4, 8, DET), f32),
             pltpu.VMEM((3, 7, 4, 8, DET), f32),

time: 86.8 us -> 84.2 us (0.970)
  Pallas kernels: 85.1 us -> 82.4 us
    pallas_call x1, Pallas kernels: 54.1 us -> 52.6 us  [reduced(): pl.pallas_call(reduce_kernel, out_shape=(jax.ShapeDtypeStruct((2, 12, 4,...]
    pallas_call x1, Pallas kernels: 9.66 us -> 8.55 us  [forward(): pl.pallas_call(forward_kernel, out_shape=(spectra, spectra, jax.ShapeDtyp...]
where the time goes in v7:
time: 84.2 us; the launch traced here: 84.1 us
  Pallas kernels  82.4 us (98%)
  local copies, waits for them, and re-layouts  0.97 us (1%)
    pallas_call x1, Pallas kernels, reduced(): pl.pallas_call(reduce_kernel, out_shape=(jax.ShapeDtypeStruct((2, 12, 4,...  52.6 us
    pallas_call x1, Pallas kernels, extended_of(): pl.pallas_call(halo_kernel, out_shape=jax.ShapeDtypeStruct((2, 3 * DET, 4...  18.7 us
    pallas_call x1, Pallas kernels, forward(): pl.pallas_call(forward_kernel, out_shape=(spectra, spectra, jax.ShapeDtyp...  8.55 us
    pallas_call x1, Pallas kernels, finished(): pl.pallas_call(finish_kernel, out_shape=(jax.ShapeDtypeStruct((24, 16, 8,...  2.64 us

profile of v7, /device:TPU:1, one launch (start us, length us, event | category | flops | bytes accessed | tf_op | source)
XLA Modules:
  0.0 84.1 jit_solution(4963064074661229983)
XLA Ops:
  0.6 0.0 copy-start.2
  0.6 0.9 %copy-done.2 = f32[2,128,256]{2,1,0:T(8,128)S(1)} copy-done((f32[2,128,256]{2,1,0:T(8,128)S(1)}, f32[2,128,256]{2,1,0:T(8,128)}, u32[]{:S(2)}) %copy-start.2) | copy-done | bytes 262168
  1.6 0.0 copy-start
  1.6 0.0 copy-start.1
  1.6 0.0 copy-start.4
  1.6 0.0 copy-start.5
  1.6 18.7 %halo.1.ext_ref = f32[2,384,512]{2,1,0:T(8,128)S(1)} custom-call(f32[2,128,256]{2,1,0:T(8,128)S(1)} %copy-done.2), custom_call_target="tpu_custom_call" | custom-call | flops 8000000000 | bytes 24000000 | tf_op jit(solution)/shard_map/halo/pallas_call | solution.py:248
  20.3 0.0 copy-done
  20.3 0.0 copy-done.1
  20.3 0.0 copy-done.4
  20.3 0.0 copy-done.5
  20.3 8.6 %forward.1 = (bf16[4,6,256,256]{3,2,1,0:T(8,128)(2,1)S(1)}, bf16[4,6,256,256]{3,2,1,0:T(8,128)(2,1)S(1)}, f32[4,2,128,128]{3,2,1,0:T(8,128)S(1)}, f32[2,128,128]{2,1,0:T(8,128)S(1)}, f32[384,512]{1,0:T(8,128)S(1)}) custom-call(s32[2,4]{1,0:T(2,128)S(1)} %bitcast.6, f32[12,2,128,128]{3,2,1,0:T(8,128)S(1)} %copy-done, f32[4,128,128]{2,1,0:T(8,128)S(1)} %copy-done.1, ...), custom_call_target="tpu_custom_call" | custom-call | flops 8999999488 | bytes 27000000 | tf_op jit(solution)/shard_map/forward/pallas_call | solution.py:144
  28.9 0.0 copy-start.3
  28.9 52.6 %reduce_all.1 = (f32[2,12,4,4,8,128]{5,4,3,2,1,0:T(8,128)S(1)}, f32[192,192]{1,0:T(8,128)S(1)}, f32[3,128,256]{2,1,0:T(8,128)S(1)}) custom-call(s32[2,4]{1,0:T(2,128)S(1)} %bitcast.7, bf16[4,6,256,256]{3,2,1,0:T(8,128)(2,1)S(1)} %get-tuple-element.12.high_ref, bf16[4,6,256,256]{3,2,1,0:T(8,128)(2,1)S(1)} %get-tuple-element.13.low_ref, ...), custom_call_target="tpu_custom_call" | custom-call | flops 44999999488 | bytes 135000000 | tf_op jit(solution)/shard_map/reduce_all/pallas_call | solution.py:554
  81.5 0.0 copy-done.3
  81.5 2.6 %finish.1 = (f32[24,16,8,128]{3,2,1,0:T(8,128)}, f32[2,128,256]{2,1,0:T(8,128)}) custom-call(f32[192,192]{1,0:T(8,128)S(1)} %get-tuple-element.17.mix_ref, f32[24,16,8,128]{3,2,1,0:T(8,128)S(1)} %bitcast.8, f32[3,128,256]{2,1,0:T(8,128)S(1)} %get-tuple-element.19.inside_ref, f32[2,128,256]{2,1,0:T(8,128)S(1)} %copy-done.3), custom_call_target="tpu_custom_call" | custom-call | flops 3000000000 | bytes 9000000 | tf_op jit(solution)/shard_map/finish/pallas_call | solution.py:651
Async XLA Ops:
  0.6 1.0 %copy-start.2 = (f32[2,128,256]{2,1,0:T(8,128)S(1)}, f32[2,128,256]{2,1,0:T(8,128)}, u32[]{:S(2)}) copy-start(f32[2,128,256]{2,1,0:T(8,128)} %spec_ref.3) | copy-start | bytes 786436
  1.6 18.7 %copy-start = (f32[12,2,128,128]{3,2,1,0:T(8,128)S(1)}, f32[12,2,128,128]{3,2,1,0:T(8,128)}, u32[]{:S(2)}) copy-start(f32[12,2,128,128]{3,2,1,0:T(8,128)} %probe_ref.1) | copy-start | bytes 4718596
  1.6 18.7 %copy-start.1 = (f32[4,128,128]{2,1,0:T(8,128)S(1)}, f32[4,128,128]{2,1,0:T(8,128)}, u32[]{:S(2)}) copy-start(f32[4,128,128]{2,1,0:T(8,128)} %patterns_ref.1) | copy-start | bytes 786436
  1.6 18.7 %copy-start.4 = (s32[4,2]{0,1:T(2,128)S(1)}, s32[4,2]{0,1:T(2,128)}, u32[]{:S(2)}) copy-start(s32[4,2]{0,1:T(2,128)} %param.8) | copy-start | bytes 100
  1.6 18.7 %copy-start.5 = (bf16[4,256,256]{2,1,0:T(8,128)(2,1)S(1)}, bf16[4,256,256]{2,1,0:T(8,128)(2,1)}, u32[]{:S(2)}) copy-start(bf16[4,256,256]{2,1,0:T(8,128)(2,1)} %constant.2.clone.tables_ref) | copy-start | bytes 1572868
  28.9 52.6 %copy-start.3 = (f32[2,128,256]{2,1,0:T(8,128)S(1)}, f32[2,128,256]{2,1,0:T(8,128)}, u32[]{:S(2)}) copy-start(f32[2,128,256]{2,1,0:T(8,128)} %spec_ref.3) | copy-start | bytes 786436
